TPU v7x, 128 devices: a whole 4x4x4 slice. The times are simulated.
128 devices in a mesh: req: 2 (over core), seq: 64 (over x, z, y).
Axes of the slice: x: 4, y: 4, z: 4, core: 2. Of those that a mesh axis runs over, the one named last changes fastest.
Arguments:
- image_query: bfloat16 [1024, 1536], P(('req', 'seq')), parts along dimension 0, may hold values from -6 to 6
- image_key: bfloat16 [1024, 1536], P(('req', 'seq')), parts along dimension 0, may hold values from -6 to 6
- image_value: bfloat16 [1024, 1536], P(('req', 'seq')), parts along dimension 0, may hold values from -6 to 6
- text_query: bfloat16 [1024, 1536], P('req'), parts along dimension 0, may hold values from -6 to 6
- text_key: bfloat16 [1024, 1536], P('req'), parts along dimension 0, may hold values from -6 to 6
- text_value: bfloat16 [1024, 1536], P('req'), parts along dimension 0, may hold values from -6 to 6
- image_query_gain: float32 [128], replicated, may hold values from 1 to 8
- image_key_gain: float32 [128], replicated, may hold values from 1 to 8
- text_query_gain: float32 [128], replicated, may hold values from 1 to 2.5
- text_key_gain: float32 [128], replicated, may hold values from 1 to 2.5
- image_order: int32 [1024], P(('req', 'seq')), parts along dimension 0, may hold values from 0 to 511, each once
- text_length: int32 [2], P('req'), parts along dimension 0, may hold values from 256 to 512
Outputs:
- image_out: bfloat16 [1024, 1536], P(('req', 'seq')), parts along dimension 0
- text_out: bfloat16 [1024, 1536], P(('req', 'seq')), parts along dimension 0
There are 2 independent parts, one for each index of `req`. A program takes and returns all parts, laid end to end along the dimension named above; an argument that names none is the same for every part. Nothing has to cross between parts.
Inputs may be any that keep to these rules, and one draw needn't show every extreme that they name: `image_order`: every position 0 to 511 appears once.
All inputs are finite; a program needn't handle non-finite values.
Results may differ from a plain program's by a relative error of at most 0.005.
The roundings to bfloat16 on the way count: a program that leaves them out, or rounds other values in their place, can miss the bound.
Values may be sent and summed in bfloat16 or wider, within the bound.
A program may use at most 64 MiB of HBM per device.

v0:
```python
import jax
import jax.numpy as jnp
from jax import lax
from jax.sharding import PartitionSpec as P

GRID_W = 64


epsilon = 1e-06
masked_score = -1e30


def in_one_piece(arrays, axis, dim, along):
    widths = [a.shape[along] for a in arrays]
    both = jnp.concatenate(arrays, axis=along)
    whole = lax.all_gather(both, axis, axis=dim, tiled=True)
    return tuple(jnp.split(whole, [sum(widths[:k]) for k in range(1, len(widths))], axis=along))


def head_norm(values, norm_gain, head_count):
    row_count = values.shape[0]
    shaped = values.astype(jnp.float32).reshape(row_count, head_count, -1)
    mean_square = jnp.mean(shaped * shaped, axis=-1, keepdims=True)
    return shaped * lax.rsqrt(mean_square + epsilon) * norm_gain


def rotate(normed, positions, half_length):
    row_count, head_count, head_dim = normed.shape
    pair_count = head_dim // 2
    pair_ids = jnp.arange(pair_count)
    first_axis = pair_ids < 8
    second = pair_ids < 36
    within = jnp.where(first_axis, pair_ids, jnp.where(second, pair_ids - 8, pair_ids - 36)).astype(
        jnp.float32
    )
    axis_dim = jnp.where(first_axis, 16.0, 56.0).astype(jnp.float32)
    frequency = jnp.power(jnp.float32(10000.0), -2.0 * within / axis_dim)
    image_index = positions // half_length
    inside = positions % half_length
    row_place = inside // GRID_W
    column_place = inside % GRID_W
    coordinate = jnp.where(
        first_axis[None, :],
        image_index[:, None],
        jnp.where(second[None, :], row_place[:, None], column_place[:, None]),
    ).astype(jnp.float32)
    angles = coordinate * frequency[None, :]
    cosine = jnp.cos(angles)[:, None, :]
    sine_part = jnp.sin(angles)[:, None, :]
    paired = normed.reshape(row_count, head_count, pair_count, 2)
    even_part = paired[..., 0]
    odd_part = paired[..., 1]
    turned = jnp.stack(
        [even_part * cosine - odd_part * sine_part, even_part * sine_part + odd_part * cosine],
        axis=-1,
    )
    return turned.reshape(row_count, head_count * head_dim)


def partial_attend(queries, key_block, value_block, key_mask, head_count):
    row_count = queries.shape[0]
    key_count = key_block.shape[0]
    query_heads = queries.reshape(row_count, head_count, -1)
    scaling = query_heads.shape[-1] ** (-0.5)
    scores = (
        jnp.einsum(
            "rhd,shd->rhs",
            query_heads,
            key_block.reshape(key_count, head_count, -1),
            preferred_element_type=jnp.float32,
        )
        * scaling
    )
    if key_mask is not None:
        scores = jnp.where(key_mask[None, None, :], scores, masked_score)
    row_max = jnp.max(scores, axis=-1)
    expo = jnp.exp(scores - row_max[..., None])
    if key_mask is not None:
        expo = jnp.where(key_mask[None, None, :], expo, 0.0)
    totals = jnp.sum(expo, axis=-1)
    blended = jnp.einsum(
        "rhs,shd->rhd",
        expo.astype(jnp.bfloat16),
        value_block.reshape(key_count, head_count, -1),
        preferred_element_type=jnp.float32,
    )
    return (row_max, totals, blended)


def combine(earlier, later):
    max_first, sum_first, out_first = earlier
    max_second, sum_second, out_second = later
    joint = jnp.maximum(max_first, max_second)
    factor_first = jnp.exp(max_first - joint)
    factor_second = jnp.exp(max_second - joint)
    return (
        joint,
        sum_first * factor_first + sum_second * factor_second,
        out_first * factor_first[..., None] + out_second * factor_second[..., None],
    )


def take_rows(state, begin, length):
    return jax.tree.map(lambda member: lax.dynamic_slice_in_dim(member, begin, length, 0), state)


def finish(state):
    row_max, totals, blended = state
    return (blended / totals[..., None]).reshape(blended.shape[0], -1).astype(jnp.bfloat16)


def local(
    image_query,
    image_key,
    image_value,
    text_query,
    text_key,
    text_value,
    image_query_gain,
    image_key_gain,
    text_query_gain,
    text_key_gain,
    image_order,
    text_length,
):
    head_size = image_query_gain.shape[0]
    head_count = image_query.shape[1] // head_size
    devices = lax.axis_size("seq")
    own_rows = image_query.shape[0]
    half_length = own_rows * devices // 2
    text_rows = text_query.shape[0]
    share = text_rows // devices
    first_row = lax.axis_index("seq") * share
    query_ready = rotate(
        head_norm(image_query, image_query_gain, head_count), image_order, half_length
    ).astype(jnp.bfloat16)
    key_ready = rotate(
        head_norm(image_key, image_key_gain, head_count), image_order, half_length
    ).astype(jnp.bfloat16)
    text_valid = jnp.arange(text_rows) < text_length[0]
    text_keys = (
        head_norm(text_key, text_key_gain, head_count).reshape(text_rows, -1).astype(jnp.bfloat16)
    )
    own_text = lax.dynamic_slice_in_dim(text_query, first_row, share, 0)
    own_ready = (
        head_norm(own_text, text_query_gain, head_count).reshape(share, -1).astype(jnp.bfloat16)
    )
    local_queries = jnp.concatenate([query_ready, own_ready], axis=0)
    text_state = partial_attend(local_queries, text_keys, text_value, text_valid, head_count)
    query_count = local_queries.shape[0]
    start_state = take_rows(text_state, 0, query_count)
    pieces = in_one_piece((key_ready, image_value), "seq", 0, 1)
    image_state = combine(
        start_state, partial_attend(local_queries, pieces[0], pieces[1], None, head_count)
    )
    image_out = finish(take_rows(image_state, 0, own_rows))
    text_out = finish(take_rows(image_state, own_rows, share))
    return (image_out, text_out)


def solution(mesh):
    placed = (
        P(("req", "seq"), None),
        P(("req", "seq"), None),
        P(("req", "seq"), None),
        P("req", None),
        P("req", None),
        P("req", None),
        P(),
        P(),
        P(),
        P(),
        P(("req", "seq")),
        P("req"),
    )
    return jax.shard_map(
        local,
        mesh=mesh,
        in_specs=placed,
        out_specs=(P(("req", "seq"), None), P(("req", "seq"), None)),
        check_vma=False,
    )
```

profile of v0, /device:TPU:1, one launch (start us, length us, event | category | flops | bytes accessed | tf_op | source)
XLA Modules:
  0.0 107.7 jit_solution(6413456446253419397)
XLA Ops:
  7.2 0.0 copy-start
  7.2 0.0 copy-start.6
  7.2 0.0 copy-start.10
  7.2 0.0 copy-start.7
  7.2 0.0 copy-start.8
  7.2 0.0 all-gather.2.cloned.1.call-start
  7.3 0.9 copy.65
  8.2 0.8 bitcast_reduce_fusion
  9.0 0.9 copy.53
  10.0 0.0 copy-done.6
  10.0 0.1 bitcast_reduce_fusion.1
  10.0 0.0 copy-done.10
  10.1 0.1 fusion.30
  10.2 0.1 copy.54
  10.3 0.1 copy.55
  10.4 0.0 copy-done.7
  10.4 0.1 mul.247
  10.5 0.0 copy-done.8
  10.5 0.1 mul.274
  10.7 0.9 multiply_multiply_fusion
  11.6 3.2 %slice_multiply_fusion.1 = (f32[8,12,64,1]{0,3,2,1:T(1,128)S(1)}, f32[8,12,64,1]{0,3,2,1:T(1,128)S(1)}, f32[8,12,64,1]{0,3,2,1:T(1,128)S(1)}, f32[8,12,64,1]{0,3...) fusion(f32[8,12,64,2]{0,3,2,1:T(2,128)S(1)} %get-tuple-element., ...), kind=kLoop, calls=%fused_computation.23 | loop fusion | flops 49152 | bytes 299008 | tf_op jit(solution)/shard_map/mul | solution.py:54
  14.8 0.2 copy.66
  15.0 0.2 copy.67
  15.3 0.2 copy.68
  15.5 0.2 copy.69
  15.8 0.3 copy.70
  16.2 0.0 copy-start.2
  16.2 0.8 copy.71
  17.0 1.4 %pad_maximum_fusion.3 = bf16[8,3072]{1,0:T(8,128)(2,1)} fusion(bf16[8,1536]{1,0:T(8,128)(2,1)} %param.14, bf16[8,1536]{1,0:T(8,128)(2,1)} %copy.71), kind=kLoop, calls=%fused_computation.47 | loop fusion | flops 98304 | bytes 98304 | tf_op jit(solution)/shard_map/concatenate | solution.py:15
  18.3 0.0 all-gather.2.cloned.1.call-update
  18.4 0.2 copy.56
  18.6 0.2 copy.57
  18.9 0.2 copy.58
  19.1 0.2 copy.59
  19.4 0.3 copy.60
  19.7 0.2 copy.61
  19.9 0.0 copy-done.2
  20.0 0.7 copy.52
  21.3 1.7 %copy.63 = bf16[512,1536]{0,1:T(8,128)(2,1)S(1)} copy(bf16[512,1536]{1,0:T(8,128)(2,1)} %param.17) | data formatting | bytes 3145728 | tf_op args[5]
  23.0 2.1 %convert_multiply_fusion.1 = f32[512,1536]{0,1:T(8,128)} fusion(bf16[512,1536]{0,1:T(8,128)(2,1)S(1)} %copy.52), kind=kLoop, calls=%fused_computation.1 | loop fusion | flops 1572864 | bytes 4718592 | tf_op jit(solution)/shard_map/mul | solution.py:23
  25.2 2.3 %reduce_sum.54 = f32[512,12]{0,1:T(8,128)S(1)} reduce(f32[512,12,128]{0,2,1:T(8,128)} %bitcast.53, f32[]{:T(128)} %constant.75.clone.1), dimensions={2}, to_apply=%region_0.0 | reduce | flops 780288 | bytes 3170308 | tf_op jit(solution)/shard_map/reduce_sum | solution.py:23
  27.4 0.0 copy-done
  27.5 0.0 copy-start.9
  27.5 0.4 fusion.1
  27.9 0.8 fusion.19
  28.7 0.0 copy-done.9
  28.8 0.8 fusion.24
  29.6 0.0 copy-start.4
  29.6 0.0 copy-done.3
  29.6 0.4 fusion.41
  30.0 0.8 fusion.10
  30.8 56.4 %all-gather.2.cloned.1.call-done = bf16[512,3072]{1,0:T(8,128)(2,1)} async-done(((bf16[8,3072]{1,0:T(8,128)(2,1)}), bf16[512,3072]{1,0:T(8,128)(2,1)}) %all-gather.2.cloned.1.call-update) | async-done | bytes 3145744 | tf_op jit(solution)/shard_map/all_gather | solution.py:16
  87.3 3.8 %fusion.38 = (bf16[512,1536]{1,0:T(8,128)(2,1)}, bf16[512,1536]{1,0:T(8,128)(2,1)}) fusion(bf16[512,3072]{1,0:T(8,128)(2,1)} %all-gather.2.cloned.1.call-done), kind=kLoop, calls=%fused_computation.93 | loop fusion | bytes 6291456 | tf_op jit(solution)/shard_map/split | solution.py:17
  91.0 0.0 copy-done.4
  91.0 1.7 %copy.80 = bf16[512,1536]{0,1:T(8,128)(2,1)S(1)} copy(bf16[512,1536]{1,0:T(8,128)(2,1)} %get-tuple-element.10) | data formatting | bytes 3145728
  92.8 2.4 %fusion.40 = (f32[16,12]{0,1:T(8,128)}, f32[16,12,512]{2,0,1:T(8,128)}) fusion(bf16[512,12,128]{0,2,1:T(8,128)(2,1)S(1)} %bitcast.57, bf16[8,12,128]{2,0,1:T(8,128)(2,1)} %copy-done.4, bf16[8,12,128]{2,0,1:T(8,128)(2,1)} %copy-done.3), kind=kOutput, calls=%fused_computation.95 | convolution fusion | flops 25460544 | bytes 2016000 | tf_op jit(solution)/shard_map/rhd,shd->rhs/dot_general | solution.py:66
  95.2 1.7 %copy.81 = bf16[512,1536]{0,1:T(8,128)(2,1)S(1)} copy(bf16[512,1536]{1,0:T(8,128)(2,1)} %get-tuple-element.9) | data formatting | bytes 3145728
  96.9 1.3 %fusion.8 = f32[16,12]{0,1:T(8,128)S(1)} fusion(f32[16,12,512]{2,0,1:T(8,128)} %get-tuple-element.34, f32[16,12]{0,1:T(8,128)} %get-tuple-element.33), kind=kLoop, calls=%fused_computation.18 | loop fusion | flops 196416 | bytes 394752 | tf_op jit(solution)/shard_map/reduce_sum | solution.py:80
  98.2 0.7 multiply_add_fusion
  98.9 0.1 fusion.39
  99.0 0.6 fusion.7
  99.6 0.0 copy-done.5
  99.6 0.6 fusion.6
  100.1 0.7 fusion.26
  (22 shorter events, 0.2 us)
Async XLA Ops:
  7.2 20.3 %copy-start = (f32[128]{0:T(128)S(1)}, f32[128]{0:T(128)}, u32[]{:S(2)}) copy-start(f32[128]{0:T(128)} %param.21) | copy-start | bytes 1540
  7.2 2.8 %copy-start.6 = (bf16[8,1536]{1,0:T(8,128)(2,1)S(1)}, bf16[8,1536]{1,0:T(8,128)(2,1)}, u32[]{:S(2)}) copy-start(bf16[8,1536]{1,0:T(8,128)(2,1)} %param.12) | copy-start | bytes 73732
  7.2 2.9 %copy-start.10 = (s32[8]{0:T(128)S(1)}, s32[8]{0:T(128)}, u32[]{:S(2)}) copy-start(s32[8]{0:T(128)} %param.22) | copy-start | bytes 100
  7.2 3.2 %copy-start.7 = (f32[128]{0:T(128)S(1)}, f32[128]{0:T(128)}, u32[]{:S(2)}) copy-start(f32[128]{0:T(128)} %param.18) | copy-start | bytes 1540
  7.2 3.3 %copy-start.8 = (f32[128]{0:T(128)S(1)}, f32[128]{0:T(128)}, u32[]{:S(2)}) copy-start(f32[128]{0:T(128)} %param.19) | copy-start | bytes 1540
  7.2 80.0 %all-gather.2.cloned.1.call-start = ((), (), s32[]{:S(2)}) async-start(), calls=%async_computation | async-start | bytes 3194880 | tf_op jit(solution)/shard_map/all_gather | solution.py:16
  16.2 3.7 %copy-start.2 = (bf16[512,1536]{1,0:T(8,128)(2,1)S(1)}, bf16[512,1536]{1,0:T(8,128)(2,1)}, u32[]{:S(2)}) copy-start(bf16[512,1536]{1,0:T(8,128)(2,1)} %param.16) | copy-start | bytes 4718596
  19.9 9.7 %copy-start.3 = (bf16[8,12,128]{2,0,1:T(8,128)(2,1)}, bf16[8,12,128]{2,0,1:T(8,128)(2,1)S(1)}, u32[]{:S(2)}) copy-start(bf16[8,12,128]{2,0,1:T(8,128)(2,1)S(1)} %copy.61) | copy-start | bytes 73732
  27.5 1.3 %copy-start.9 = (f32[128]{0:T(128)S(1)}, f32[128]{0:T(128)}, u32[]{:S(2)}) copy-start(f32[128]{0:T(128)} %param.20) | copy-start | bytes 1540
  29.6 61.4 %copy-start.4 = (bf16[8,12,128]{2,0,1:T(8,128)(2,1)}, bf16[8,12,128]{2,0,1:T(8,128)(2,1)S(1)}, u32[]{:S(2)}) copy-start(bf16[8,12,128]{2,0,1:T(8,128)(2,1)S(1)} %fusion.24) | copy-start | bytes 73732
  96.9 2.6 %copy-start.1 = (f32[16,12,512]{2,0,1:T(8,128)S(1)}, f32[16,12,512]{2,0,1:T(8,128)}, u32[]{:S(2)}) copy-start(f32[16,12,512]{2,0,1:T(8,128)} %get-tuple-element.34) | copy-start | bytes 1179652
  96.9 2.7 %copy-start.5 = (f32[16,12]{0,1:T(8,128)S(1)}, f32[16,12]{0,1:T(8,128)}, u32[]{:S(2)}) copy-start(f32[16,12]{0,1:T(8,128)} %get-tuple-element.33) | copy-start | bytes 2308
Sparse Core Ops, SparseCore 0:
  18.5 68.7 all-gather.1
where the time goes:
time: 109 us; the launch traced here: 108 us
  waiting for transfers between devices  56.4 us (52%)
  other arithmetic  16.6 us (15%)
  local copies, waits for them, and re-layouts  15.6 us (14%)
  between operations  15.1 us (14%)
  matrix products  3.94 us (4%)
    all_gather x1, waiting for transfers between devices, in_one_piece(): whole = lax.all_gather(both, axis, axis=dim, tiled=True)  56.4 us
    unnamed x26, local copies, waits for them, and re-layouts  5.92 us
    reduce_sum x4, other arithmetic, head_norm(): mean_square = jnp.mean(shaped * shaped, axis=-1, keepdims=True)  4 us
    split x1, local copies, waits for them, and re-layouts, in_one_piece(): jnp.split(whole, [sum(widths[:k]) for k in range(1, len(widths))], axis=a...  3.76 us
    mul x1, other arithmetic, rotate(): odd_part * sine_part  3.16 us
    dot_general x2, matrix products, partial_attend(): jnp.einsum('rhd,shd->rhs', query_heads, key_block.reshape(key_count, head...  2.82 us
  transfers between devices with their start and end apart: 1, of which 1 were waited for; matrix products, arithmetic and copies ran while one was open for 11% of the time, Pallas kernels for 0%

commit v1 on v0

v1 whole, which is shorter than its diff:
```python
import jax
import jax.numpy as jnp
from jax import lax
from jax.experimental import pallas as pl
from jax.experimental.pallas import tpu as pltpu
from jax.sharding import PartitionSpec as P

GRID_W = 64
EPS = 1e-06
NEG = -1e30
MESH = pl.DeviceIdType.MESH
HEADS = 12
HD = 128
ROWS = 8
PLANE = 16
SEQ = 64
LOG2E = 1.4426950408889634

OFFSETS = [(2, 2), (2, 1), (2, 3), (1, 2), (3, 2), (1, 1), (1, 3), (3, 1), (3, 3), (2, 0), (0, 2),
           (1, 0), (3, 0), (0, 1), (0, 3), (0, 0)]


def normed(x, gain):
    mean_square = jnp.mean(x * x, axis=-1, keepdims=True)
    return x * lax.rsqrt(mean_square + EPS) * gain


def rotary(order_ref):
    row = lax.broadcasted_iota(jnp.int32, (ROWS, HD), 0)
    lane = lax.broadcasted_iota(jnp.int32, (ROWS, HD), 1)
    position = jnp.zeros((ROWS, HD), jnp.int32)
    for r in range(ROWS):
        position = jnp.where(row == r, order_ref[r], position)
    pair = lane >> 1
    first = pair < 8
    second = pair < 36
    within = jnp.where(first, pair, jnp.where(second, pair - 8, pair - 36)).astype(jnp.float32)
    width = jnp.where(first, 16.0, 56.0).astype(jnp.float32)
    frequency = jnp.exp(within / width * jnp.float32(-2.0 * 9.210340371976184))
    half = 4 * GRID_W
    inside = position & (half - 1)
    place = jnp.where(first, position >> 8, jnp.where(second, inside >> 6, inside & (GRID_W - 1)))
    angle = place.astype(jnp.float32) * frequency
    even = (lane & 1) == 0
    sine = jnp.sin(angle)
    return jnp.cos(angle), jnp.where(even, -sine, sine), even


def turn(x, cosine, sine, even):
    other = jnp.where(even, pltpu.roll(x, HD - 1, 1), pltpu.roll(x, 1, 1))
    return x * cosine + other * sine


def scores_of(q, k):
    return lax.dot_general(q, k, (((1,), (1,)), ((), ())), preferred_element_type=jnp.float32)


def kernel(order_ref, length_ref, iq_hbm, ik_hbm, iv_hbm, tq_hbm, tk_hbm, tv_hbm, gains_hbm,
           image_out, text_out,
           iq, ik, iv, tq, tk, tv, gains, kv_out, q_out, kv_in, q_in, o_out, o_in,
           load_sem, kv_send, kv_recv, q_send, q_recv, o_send, o_recv):
    me = lax.axis_index("seq")
    x, z, y = me // 16, (me // 4) % 4, me % 4
    spot = me % PLANE
    slot = (y - z + 3) % 4
    owner = slot < 3
    head = z * 3 + jnp.minimum(slot, 2)
    scale = HD ** -0.5 * LOG2E

    barrier = pltpu.get_barrier_semaphore()

    def greet(i, c):
        pl.semaphore_signal(barrier, inc=1, device_id={"seq": (me + i) % SEQ}, device_id_type=MESH)
        return c

    lax.fori_loop(1, SEQ, greet, 0)

    column = pl.ds(pl.multiple_of(head * HD, HD), HD)
    loads = [
        pltpu.make_async_copy(ik_hbm, ik, load_sem.at[0]),
        pltpu.make_async_copy(iv_hbm, iv, load_sem.at[1]),
        pltpu.make_async_copy(iq_hbm, iq, load_sem.at[2]),
        pltpu.make_async_copy(gains_hbm, gains, load_sem.at[3]),
        pltpu.make_async_copy(tk_hbm.at[:, column], tk, load_sem.at[4]),
        pltpu.make_async_copy(
            tq_hbm.at[pl.ds(pl.multiple_of(x * 128, 128), 128), column], tq, load_sem.at[5]),
        pltpu.make_async_copy(tv_hbm.at[:, column], tv, load_sem.at[6]),
    ]
    for load in loads:
        load.start()
    cosine, sine, even = rotary(order_ref)
    for load in loads[:4]:
        load.wait()

    for h in range(HEADS):
        cols = slice(h * HD, (h + 1) * HD)
        k = turn(normed(ik[:, cols].astype(jnp.float32), gains[1:2, :]), cosine, sine, even)
        v = iv[:, cols].astype(jnp.float32)
        kv_out[h] = jnp.concatenate([k, v], axis=0).astype(jnp.bfloat16)
        q = turn(normed(iq[:, cols].astype(jnp.float32), gains[0:1, :]), cosine, sine, even)
        q_out[h] = q.astype(jnp.bfloat16).astype(jnp.float32)

    pl.semaphore_wait(barrier, SEQ - 1)

    js = [(j + y) % 3 for j in range(3)]

    def kv_copy(h, to):
        return pltpu.make_async_remote_copy(
            src_ref=kv_out.at[h], dst_ref=kv_in.at[me], send_sem=kv_send, recv_sem=kv_recv,
            device_id={"seq": to}, device_id_type=MESH)

    def q_copy(h, to):
        return pltpu.make_async_remote_copy(
            src_ref=q_out.at[h], dst_ref=q_in.at[spot], send_sem=q_send, recv_sem=q_recv,
            device_id={"seq": to}, device_id_type=MESH)

    def owners(dx, dz):
        tx, tz = (x + dx) % 4, (z + dz) % 4
        for j in js:
            yield tz * 3 + j, tx * 16 + tz * 4 + (tz + 1 + j) % 4

    for dx, dz in OFFSETS:
        for h, to in owners(dx, dz):
            if dx == 0 and dz == 0:
                @pl.when(to != me)
                def _():
                    kv_copy(h, to).start()
                    q_copy(h, to).start()
            else:
                kv_copy(h, to).start()
                if dx == 0:
                    q_copy(h, to).start()

    @pl.when(owner)
    def _():
        kv_in[me] = kv_out[head]
        q_in[spot] = q_out[head]
        for load in loads[4:]:
            load.wait()
        keys = normed(tk[...].astype(jnp.float32), gains[3:4, :]).astype(jnp.bfloat16)
        text_queries = normed(tq[...].astype(jnp.float32), gains[2:3, :])
        pltpu.make_async_copy(q_in.at[pl.ds(0, PLANE - 1)], q_in.at[pl.ds(0, PLANE - 1)], q_recv).wait()
        q = jnp.concatenate([q_in[...], text_queries.reshape(PLANE, ROWS, HD)], axis=1)
        q = q.reshape(PLANE * 2 * ROWS, HD).astype(jnp.bfloat16)
        s = scores_of(q, keys)
        valid = lax.broadcasted_iota(jnp.int32, s.shape, 1) < length_ref[0]
        s = jnp.where(valid, s, NEG)
        text_max = jnp.max(s, axis=-1, keepdims=True)
        e = jnp.exp2((s - text_max) * scale)
        text_sum = jnp.sum(e, axis=-1, keepdims=True)
        text_part = jnp.dot(e.astype(jnp.bfloat16), tv[...], preferred_element_type=jnp.float32)

        pltpu.make_async_copy(kv_in.at[pl.ds(0, SEQ - 1)], kv_in.at[pl.ds(0, SEQ - 1)], kv_recv).wait()
        kv = kv_in[...].astype(jnp.float32)
        k = kv[:, :ROWS, :].reshape(SEQ * ROWS, HD).astype(jnp.bfloat16)
        v = kv[:, ROWS:, :].reshape(SEQ * ROWS, HD).astype(jnp.bfloat16)
        s = scores_of(q, k)
        top = jnp.maximum(jnp.max(s, axis=-1, keepdims=True), text_max)
        e = jnp.exp2((s - top) * scale)
        keep = jnp.exp2((text_max - top) * scale)
        total = jnp.sum(e, axis=-1, keepdims=True) + text_sum * keep
        o = jnp.dot(e.astype(jnp.bfloat16), v, preferred_element_type=jnp.float32) + text_part * keep
        o = (o / total).astype(jnp.bfloat16)
        o_out[...] = o.reshape(PLANE, 2 * ROWS, HD)
        for i in range(1, PLANE):
            other = (spot + i) % PLANE
            pltpu.make_async_remote_copy(
                src_ref=o_out.at[other], dst_ref=o_in.at[head], send_sem=o_send, recv_sem=o_recv,
                device_id={"seq": x * 16 + other}, device_id_type=MESH).start()
        o_in[head] = o_out[spot]
        pltpu.make_async_copy(o_in.at[pl.ds(0, HEADS - 1)], o_in.at[pl.ds(0, HEADS - 1)], o_recv).wait()

    @pl.when(jnp.logical_not(owner))
    def _():
        for load in loads[4:]:
            load.wait()
        pltpu.make_async_copy(o_in, o_in, o_recv).wait()

    for h in range(HEADS):
        o = o_in[h].astype(jnp.float32)
        cols = slice(h * HD, (h + 1) * HD)
        image_out[:, cols] = o[:ROWS].astype(jnp.bfloat16)
        text_out[:, cols] = o[ROWS:].astype(jnp.bfloat16)

    def drain(ref, count, sem):
        pltpu.make_async_copy(ref.at[pl.ds(0, count)], ref.at[pl.ds(0, count)], sem).wait()

    drain(kv_in, 47, kv_send)
    drain(q_in, 11, q_send)

    @pl.when(owner)
    def _():
        drain(o_out, PLANE - 1, o_send)

    @pl.when(jnp.logical_not(owner))
    def _():
        drain(kv_in, 1, kv_send)
        drain(q_in, 1, q_send)


def local(image_query, image_key, image_value, text_query, text_key, text_value, image_query_gain,
          image_key_gain, text_query_gain, text_key_gain, image_order, text_length):
    gains = jnp.stack([image_query_gain, image_key_gain, text_query_gain, text_key_gain])
    hbm = pl.BlockSpec(memory_space=pl.ANY)
    smem = pl.BlockSpec(memory_space=pltpu.SMEM)
    vmem = pl.BlockSpec(memory_space=pltpu.VMEM)
    bf16, f32 = jnp.bfloat16, jnp.float32
    width = image_query.shape[1]
    text_rows = text_key.shape[0]
    out = jax.ShapeDtypeStruct((ROWS, width), bf16)
    dma = pltpu.SemaphoreType.DMA
    return pl.pallas_call(
        kernel,
        out_shape=(out, out),
        in_specs=[smem, smem] + [hbm] * 7,
        out_specs=(vmem, vmem),
        scratch_shapes=[
            pltpu.VMEM((ROWS, width), bf16),
            pltpu.VMEM((ROWS, width), bf16),
            pltpu.VMEM((ROWS, width), bf16),
            pltpu.VMEM((PLANE * ROWS, HD), bf16),
            pltpu.VMEM((text_rows, HD), bf16),
            pltpu.VMEM((text_rows, HD), bf16),
            pltpu.VMEM((4, HD), f32),
            pltpu.VMEM((HEADS, 2 * ROWS, HD), bf16),
            pltpu.VMEM((HEADS, ROWS, HD), f32),
            pltpu.VMEM((SEQ, 2 * ROWS, HD), bf16),
            pltpu.VMEM((PLANE, ROWS, HD), f32),
            pltpu.VMEM((PLANE, 2 * ROWS, HD), bf16),
            pltpu.VMEM((HEADS, 2 * ROWS, HD), bf16),
            dma((7,)), dma, dma, dma, dma, dma, dma,
        ],
        compiler_params=pltpu.CompilerParams(collective_id=0, has_side_effects=True),
        name="joint",
    )(image_order, text_length, image_query, image_key, image_value, text_query, text_key, text_value, gains)


def solution(mesh):
    placed = (
        P(("req", "seq"), None),
        P(("req", "seq"), None),
        P(("req", "seq"), None),
        P("req", None),
        P("req", None),
        P("req", None),
        P(),
        P(),
        P(),
        P(),
        P(("req", "seq")),
        P("req"),
    )
    return jax.shard_map(
        local,
        mesh=mesh,
        in_specs=placed,
        out_specs=(P(("req", "seq"), None), P(("req", "seq"), None)),
        check_vma=False,
    )
```

time: 109 us -> 27.6 us (0.25)
  the two profiles are of different devices: /device:TPU:1 before, /device:TPU:0 now
where the time goes in v1:
time: 27.6 us; the launch traced here: 27.4 us
  Pallas kernels  22.1 us (80%)
  local copies, waits for them, and re-layouts  2.69 us (10%)
  other arithmetic  1.29 us (5%)
  between operations  1.29 us (5%)
    pallas_call x1, Pallas kernels, local(): pl.pallas_call(kernel, out_shape=(out, out), in_specs=[smem, smem] + [hbm...  22.1 us
    unnamed x2, local copies, waits for them, and re-layouts  2.69 us
    another operation x1, other arithmetic, local(): jnp.stack([image_query_gain, image_key_gain, text_query_gain, text_key_ga...  1.29 us

profile of v1, /device:TPU:0, one launch (start us, length us, event | category | flops | bytes accessed | tf_op | source)
XLA Modules:
  0.0 27.4 jit_solution(30909564746751832)
XLA Ops:
  1.3 1.3 %pad_maximum_fusion.gains_hbm = f32[4,128]{1,0:T(4,128)} fusion(f32[1,128]{1,0:T(1,128)} %bitcast.4, f32[1,128]{1,0:T(1,128)} %bitcast.5, f32[1,128]{1,0:T(1,128)} %bitcast.6, f32[1,128]{1,0:T(1,128)} %bitcast.7), kind=kLoop, calls=%fused_computation | loop fusion | flops 1536 | bytes 4096 | tf_op jit(solution)/shard_map/stack | solution.py:203
  2.6 22.1 %joint.1 = (bf16[8,1536]{1,0:T(8,128)(2,1)}, bf16[8,1536]{1,0:T(8,128)(2,1)}) custom-call(s32[8]{0:T(128)} %order_ref.1, s32[1]{0:T(128)S(6)} %copy.16.length_ref, bf16[8,1536]{1,0:T(8,128)(2,1)} %iq_hbm.1, bf16[8,1536]{1,0:T(8,128)(2,1)} %ik_hbm.1, bf16[8,1536]{1,0:T(8,128)(2,1)} %iv_hbm.1, bf16[512,1536]{1,0:T(8,128)(2,1)} %tq_hbm.1, ...), custom_call_target="tpu_custom_call" | custom-call | tf_op jit(solution)/shard_map/joint/pallas_call | solution.py:212
  24.7 1.3 %copy.17 = bf16[8,1536]{1,0:T(8,128)(2,1)} copy(bf16[8,1536]{1,0:T(8,128)(2,1)} %get-tuple-element.4) | data formatting | bytes 49152
  26.0 1.3 %copy.18 = bf16[8,1536]{1,0:T(8,128)(2,1)} copy(bf16[8,1536]{1,0:T(8,128)(2,1)} %get-tuple-element.5) | data formatting | bytes 49152

commit v2 on v1

v2 whole, which is shorter than its diff:
```python
import jax
import jax.numpy as jnp
from jax import lax
from jax.experimental import pallas as pl
from jax.experimental.pallas import tpu as pltpu
from jax.sharding import PartitionSpec as P

GRID_W = 64
EPS = 1e-06
NEG = -1e30
MESH = pl.DeviceIdType.MESH
HEADS = 12
HD = 128
ROWS = 8
PLANE = 16
SEQ = 64
LOG2E = 1.4426950408889634


def at(x, z, y):
    return x * 16 + z * 4 + y


OWNERS = [at(0, 0, 0), at(0, 3, 0), at(1, 0, 0), at(1, 3, 0), at(0, 0, 1), at(0, 3, 1),
          at(3, 0, 0), at(3, 3, 0), at(0, 0, 3), at(0, 3, 3), at(2, 0, 0), at(0, 0, 2)]


def normed(x, gain):
    mean_square = jnp.mean(x * x, axis=-1, keepdims=True)
    return x * lax.rsqrt(mean_square + EPS) * gain


def lanes():
    lane = lax.broadcasted_iota(jnp.int32, (ROWS, HD), 1)
    pair = lane >> 1
    first = pair < 8
    second = pair < 36
    within = jnp.where(first, pair, jnp.where(second, pair - 8, pair - 36)).astype(jnp.float32)
    width = jnp.where(first, 16.0, 56.0).astype(jnp.float32)
    frequency = jnp.exp(within / width * jnp.float32(-2.0 * 9.210340371976184))
    return frequency, first, second, (lane & 1) == 0


def rotary(order_ref, frequency, first, second, even):
    row = lax.broadcasted_iota(jnp.int32, (ROWS, HD), 0)
    position = jnp.zeros((ROWS, HD), jnp.int32)
    for r in range(ROWS):
        position = jnp.where(row == r, order_ref[r], position)
    half = 4 * GRID_W
    inside = position & (half - 1)
    place = jnp.where(first, position >> 8, jnp.where(second, inside >> 6, inside & (GRID_W - 1)))
    angle = place.astype(jnp.float32) * frequency
    sine = jnp.sin(angle)
    return jnp.cos(angle), jnp.where(even, -sine, sine)


def turn(x, cosine, sine, even):
    other = jnp.where(even, pltpu.roll(x, HD - 1, 1), pltpu.roll(x, 1, 1))
    return x * cosine + other * sine


def scores_of(q, k):
    return lax.dot_general(q, k, (((1,), (1,)), ((), ())), preferred_element_type=jnp.float32)


def kernel(order_hbm, length_ref, iq_hbm, ik_hbm, iv_hbm, tq_hbm, tk_hbm, tv_hbm,
           iq_gain_hbm, ik_gain_hbm, tq_gain_hbm, tk_gain_hbm,
           o_in,
           order, iq, ik, iv, tq, tk, tv, gains, kv_out, q_out, kv_in, q_in, o_out,
           load_sem, kv_send, kv_recv, q_send, q_recv, o_send, o_recv):
    me = lax.axis_index("seq")
    x, z, y = me // 16, (me // 4) % 4, me % 4
    spot = z * 16 + x * 4 + y
    head = jnp.int32(0)
    owner = me == OWNERS[0]
    for h in range(1, HEADS):
        mine = me == OWNERS[h]
        head = jnp.where(mine, h, head)
        owner = jnp.logical_or(owner, mine)
    scale = HD ** -0.5 * LOG2E

    loads = [
        pltpu.make_async_copy(order_hbm, order, load_sem.at[0]),
        pltpu.make_async_copy(ik_hbm, ik, load_sem.at[1]),
        pltpu.make_async_copy(ik_gain_hbm, gains.at[1:2], load_sem.at[2]),
        pltpu.make_async_copy(iv_hbm, iv, load_sem.at[3]),
        pltpu.make_async_copy(iq_hbm, iq, load_sem.at[4]),
        pltpu.make_async_copy(iq_gain_hbm, gains.at[0:1], load_sem.at[5]),
    ]
    for load in loads:
        load.start()
    barrier = pltpu.get_barrier_semaphore()
    column = pl.ds(pl.multiple_of(head * HD, HD), HD)
    text_loads = [
        pltpu.make_async_copy(tk_gain_hbm, gains.at[3:4], load_sem.at[6]),
        pltpu.make_async_copy(tk_hbm.at[:, column], tk, load_sem.at[7]),
        pltpu.make_async_copy(tq_gain_hbm, gains.at[2:3], load_sem.at[8]),
        pltpu.make_async_copy(tq_hbm.at[:, column], tq, load_sem.at[9]),
        pltpu.make_async_copy(tv_hbm.at[:, column], tv, load_sem.at[10]),
    ]

    @pl.when(owner)
    def _():
        def greet(i, c):
            pl.semaphore_signal(barrier, inc=1, device_id={"seq": (me + i) % SEQ}, device_id_type=MESH)
            return c

        lax.fori_loop(1, SEQ, greet, 0)
        for load in text_loads:
            load.start()

    frequency, first, second, even = lanes()
    loads[0].wait()
    cosine, sine = rotary(order, frequency, first, second, even)
    for load in loads[1:4]:
        load.wait()

    for h in range(HEADS):
        cols = slice(h * HD, (h + 1) * HD)
        k = turn(normed(ik[:, cols].astype(jnp.float32), gains[1:2, :]), cosine, sine, even)
        v = iv[:, cols].astype(jnp.float32)
        kv_out[h] = jnp.concatenate([k, v], axis=0).astype(jnp.bfloat16)

    @pl.when(owner)
    def _():
        pl.semaphore_wait(barrier, HEADS - 1)

    @pl.when(jnp.logical_not(owner))
    def _():
        pl.semaphore_wait(barrier, HEADS)

    for h in range(HEADS):
        @pl.when(me != OWNERS[h])
        def _():
            pltpu.make_async_remote_copy(
                src_ref=kv_out.at[h], dst_ref=kv_in.at[spot], send_sem=kv_send, recv_sem=kv_recv.at[z],
                device_id={"seq": OWNERS[h]}, device_id_type=MESH).start()

    for load in loads[4:]:
        load.wait()
    for h in range(HEADS):
        cols = slice(h * HD, (h + 1) * HD)
        q = turn(normed(iq[:, cols].astype(jnp.float32), gains[0:1, :]), cosine, sine, even)
        q_out[h] = q.astype(jnp.bfloat16)
    for h in range(HEADS):
        @pl.when(me != OWNERS[h])
        def _():
            pltpu.make_async_remote_copy(
                src_ref=q_out.at[h], dst_ref=q_in.at[spot], send_sem=q_send, recv_sem=q_recv.at[z],
                device_id={"seq": OWNERS[h]}, device_id_type=MESH).start()

    def drain(ref, count, sem):
        pltpu.make_async_copy(ref.at[pl.ds(0, count)], ref.at[pl.ds(0, count)], sem).wait()

    def arrived(ref, sem, group):
        @pl.when(z == group)
        def _():
            drain(ref, PLANE - 1, sem.at[group])

        @pl.when(z != group)
        def _():
            drain(ref, PLANE, sem.at[group])

    @pl.when(owner)
    def _():
        kv_in[spot] = kv_out[head]
        q_in[spot] = q_out[head]
        for load in text_loads:
            load.wait()
        text_keys = normed(tk[...].astype(jnp.float32), gains[3:4, :]).astype(jnp.bfloat16)
        text_queries = normed(tq[...].astype(jnp.float32), gains[2:3, :])
        text_values = tv[...]

        def queries(group):
            image = q_in[pl.ds(group * PLANE, PLANE)].astype(jnp.float32)
            text = jnp.concatenate(
                [text_queries[i * 128 + group * 32:i * 128 + group * 32 + 32] for i in range(4)], axis=0)
            both = jnp.concatenate([image, text.reshape(PLANE, ROWS, HD)], axis=1)
            return both.reshape(PLANE * 2 * ROWS, HD).astype(jnp.bfloat16)

        def text_part(q):
            s = scores_of(q, text_keys)
            valid = lax.broadcasted_iota(jnp.int32, s.shape, 1) < length_ref[0]
            s = jnp.where(valid, s, NEG)
            top = jnp.max(s, axis=-1, keepdims=True)
            e = jnp.exp2((s - top) * scale)
            total = jnp.sum(e, axis=-1, keepdims=True)
            return top, total, jnp.dot(e.astype(jnp.bfloat16), text_values, preferred_element_type=jnp.float32)

        early = {}
        for group in (0, 1):
            arrived(q_in, q_recv, group)
            q = queries(group)
            early[group] = (q, text_part(q))
        for group in range(4):
            arrived(kv_in, kv_recv, group)
        kv = kv_in[...].astype(jnp.float32)
        k = kv[:, :ROWS, :].reshape(SEQ * ROWS, HD).astype(jnp.bfloat16)
        v = kv[:, ROWS:, :].reshape(SEQ * ROWS, HD).astype(jnp.bfloat16)
        for group in (0, 1, 3, 2):
            if group not in early:
                arrived(q_in, q_recv, group)
                q = queries(group)
                early[group] = (q, text_part(q))
            q, (text_max, text_sum, text_out) = early[group]
            s = scores_of(q, k)
            top = jnp.maximum(jnp.max(s, axis=-1, keepdims=True), text_max)
            e = jnp.exp2((s - top) * scale)
            keep = jnp.exp2((text_max - top) * scale)
            total = jnp.sum(e, axis=-1, keepdims=True) + text_sum * keep
            o = jnp.dot(e.astype(jnp.bfloat16), v, preferred_element_type=jnp.float32) + text_out * keep
            o = (o / total).astype(jnp.bfloat16)
            o_out[pl.ds(group * PLANE, PLANE)] = o.reshape(PLANE, 2 * ROWS, HD)
            for i in range(PLANE):
                to = at(i // 4, group, i % 4)

                def send():
                    pltpu.make_async_remote_copy(
                        src_ref=o_out.at[group * PLANE + i], dst_ref=o_in.at[head], send_sem=o_send,
                        recv_sem=o_recv, device_id={"seq": to}, device_id_type=MESH).start()

                if to in OWNERS:
                    pl.when(me != to)(send)
                else:
                    send()
        o_in[head] = o_out[spot]
        drain(o_in, HEADS - 1, o_recv)
        drain(kv_out, HEADS - 1, kv_send)
        drain(q_out, HEADS - 1, q_send)
        drain(o_out, SEQ - 1, o_send)

    @pl.when(jnp.logical_not(owner))
    def _():
        drain(o_in, HEADS, o_recv)
        drain(kv_out, HEADS, kv_send)
        drain(q_out, HEADS, q_send)


def spread(o_in, image_hbm, text_hbm, image, text, sem):
    for h in range(HEADS):
        o = o_in[h].astype(jnp.float32)
        cols = slice(h * HD, (h + 1) * HD)
        image[:, cols] = o[:ROWS].astype(jnp.bfloat16)
        text[:, cols] = o[ROWS:].astype(jnp.bfloat16)
    stores = [pltpu.make_async_copy(image, image_hbm, sem.at[0]), pltpu.make_async_copy(text, text_hbm, sem.at[1])]
    for store in stores:
        store.start()
    for store in stores:
        store.wait()


def local(image_query, image_key, image_value, text_query, text_key, text_value, image_query_gain,
          image_key_gain, text_query_gain, text_key_gain, image_order, text_length):
    hbm = pl.BlockSpec(memory_space=pl.ANY)
    smem = pl.BlockSpec(memory_space=pltpu.SMEM)
    vmem = pl.BlockSpec(memory_space=pltpu.VMEM)
    bf16, f32 = jnp.bfloat16, jnp.float32
    width = image_query.shape[1]
    text_rows = text_key.shape[0]
    dma = pltpu.SemaphoreType.DMA
    gains = [g.reshape(1, HD) for g in (image_query_gain, image_key_gain, text_query_gain, text_key_gain)]
    blocks = pl.pallas_call(
        kernel,
        out_shape=pltpu.VMEM((HEADS, 2 * ROWS, HD), bf16),
        in_specs=[hbm, smem] + [hbm] * 10,
        out_specs=vmem,
        scratch_shapes=[
            pltpu.SMEM((ROWS,), jnp.int32),
            pltpu.VMEM((ROWS, width), bf16),
            pltpu.VMEM((ROWS, width), bf16),
            pltpu.VMEM((ROWS, width), bf16),
            pltpu.VMEM((text_rows, HD), bf16),
            pltpu.VMEM((text_rows, HD), bf16),
            pltpu.VMEM((text_rows, HD), bf16),
            pltpu.VMEM((4, HD), f32),
            pltpu.VMEM((HEADS, 2 * ROWS, HD), bf16),
            pltpu.VMEM((HEADS, ROWS, HD), bf16),
            pltpu.VMEM((SEQ, 2 * ROWS, HD), bf16),
            pltpu.VMEM((SEQ, ROWS, HD), bf16),
            pltpu.VMEM((SEQ, 2 * ROWS, HD), bf16),
            dma((11,)), dma, dma((4,)), dma, dma((4,)), dma, dma,
        ],
        compiler_params=pltpu.CompilerParams(collective_id=0, has_side_effects=True),
        name="joint",
    )(image_order, text_length, image_query, image_key, image_value, text_query, text_key, text_value, *gains)
    out = jax.ShapeDtypeStruct((ROWS, width), bf16)
    return pl.pallas_call(
        spread,
        out_shape=(out, out),
        in_specs=[vmem],
        out_specs=(hbm, hbm),
        scratch_shapes=[pltpu.VMEM((ROWS, width), bf16), pltpu.VMEM((ROWS, width), bf16), dma((2,))],
        name="spread",
    )(pltpu.with_memory_space_constraint(blocks, pltpu.VMEM))


def solution(mesh):
    placed = (
        P(("req", "seq"), None),
        P(("req", "seq"), None),
        P(("req", "seq"), None),
        P("req", None),
        P("req", None),
        P("req", None),
        P(),
        P(),
        P(),
        P(),
        P(("req", "seq")),
        P("req"),
    )
    return jax.shard_map(
        local,
        mesh=mesh,
        in_specs=placed,
        out_specs=(P(("req", "seq"), None), P(("req", "seq"), None)),
        check_vma=False,
    )
```

time: 27.6 us -> 23.2 us (0.84)
  the two profiles are of different devices: /device:TPU:0 before, /device:TPU:4 now
where the time goes in v2:
time: 23.2 us; the launch traced here: 23 us
  Pallas kernels  21.7 us (94%)
  between operations  1.29 us (6%)
    pallas_call x1, Pallas kernels, local(): pl.pallas_call(kernel, out_shape=pltpu.VMEM((HEADS, 2 * ROWS, HD), bf16),...  21.1 us
    pallas_call x1, Pallas kernels, local(): pl.pallas_call(spread, out_shape=(out, out), in_specs=[vmem], out_specs=(...  0.64 us

profile of v2, /device:TPU:4, one launch (start us, length us, event | category | flops | bytes accessed | tf_op | source)
XLA Modules:
  0.0 23.0 jit_solution(14927197701844385892)
XLA Ops:
  1.3 21.1 %joint.1.o_in = bf16[12,16,128]{2,1,0:T(8,128)(2,1)S(1)} custom-call(s32[8]{0:T(128)} %order_hbm.1, s32[1]{0:T(128)S(6)} %copy.14.length_ref, bf16[8,1536]{1,0:T(8,128)(2,1)} %iq_hbm.1, bf16[8,1536]{1,0:T(8,128)(2,1)} %ik_hbm.1, bf16[8,1536]{1,0:T(8,128)(2,1)} %iv_hbm.1, bf16[512,1536]{1,0:T(8,128)(2,1)} %tq_hbm.1, bf16[512,1536]{1,0:T(8,128)(2,1)} %tk_hbm.1, ...), custom_call_target="tpu_custom_call" | custom-call | tf_op jit(solution)/shard_map/joint/pallas_call | solution.py:262
  22.4 0.6 %spread.1 = (bf16[8,1536]{1,0:T(8,128)(2,1)}, bf16[8,1536]{1,0:T(8,128)(2,1)}) custom-call(bf16[12,16,128]{2,1,0:T(8,128)(2,1)S(1)} %joint.1.o_in), custom_call_target="tpu_custom_call" | custom-call | tf_op jit(solution)/shard_map/spread/pallas_call | solution.py:287

commit v3 on v2

--- a/solution.py
+++ b/solution.py
@@ -21,8 +21,20 @@
     return x * 16 + z * 4 + y
 
 
-OWNERS = [at(0, 0, 0), at(0, 3, 0), at(1, 0, 0), at(1, 3, 0), at(0, 0, 1), at(0, 3, 1),
-          at(3, 0, 0), at(3, 3, 0), at(0, 0, 3), at(0, 3, 3), at(2, 0, 0), at(0, 0, 2)]
+OWNERS = (
+    [at(0, 0, 0), at(1, 0, 0), at(0, 0, 1), at(0, 1, 0), at(1, 0, 1), at(1, 1, 0),
+     at(0, 1, 1), at(2, 0, 0), at(0, 0, 2), at(0, 2, 0), at(1, 1, 1), at(3, 0, 0)],
+    [at(0, 0, 3), at(1, 0, 2), at(2, 0, 1), at(3, 0, 1), at(1, 0, 3), at(2, 0, 2),
+     at(2, 1, 0), at(0, 1, 2), at(3, 1, 0), at(0, 1, 3), at(1, 1, 2), at(2, 1, 1)],
+)
+OWNING = set(OWNERS[0] + OWNERS[1])
+
+
+def ring(a):
+    return min(a, 4 - a)
+
+
+FAR_FIRST = sorted(range(SEQ), key=lambda t: -(ring(t // 16) + 1.5 * ring(t // 4 % 4) + ring(t % 4)))
 
 
 def normed(x, gain):
@@ -71,10 +83,12 @@
     me = lax.axis_index("seq")
     x, z, y = me // 16, (me // 4) % 4, me % 4
     spot = z * 16 + x * 4 + y
+    other_request = lax.axis_index("req") == 1
+    owners = [jnp.where(other_request, b, a) for a, b in zip(*OWNERS)]
     head = jnp.int32(0)
-    owner = me == OWNERS[0]
+    owner = me == owners[0]
     for h in range(1, HEADS):
-        mine = me == OWNERS[h]
+        mine = me == owners[h]
         head = jnp.where(mine, h, head)
         owner = jnp.logical_or(owner, mine)
     scale = HD ** -0.5 * LOG2E
@@ -101,40 +115,45 @@
 
     @pl.when(owner)
     def _():
-        def greet(i, c):
-            pl.semaphore_signal(barrier, inc=1, device_id={"seq": (me + i) % SEQ}, device_id_type=MESH)
-            return c
-
-        lax.fori_loop(1, SEQ, greet, 0)
+        with jax.named_scope("b_greet"):
+            for t in FAR_FIRST:
+                def greet():
+                    pl.semaphore_signal(barrier, inc=1, device_id={"seq": t}, device_id_type=MESH)
+
+                if t in OWNING:
+                    pl.when(me != t)(greet)
+                else:
+                    greet()
         for load in text_loads:
             load.start()
 
     frequency, first, second, even = lanes()
-    loads[0].wait()
-    cosine, sine = rotary(order, frequency, first, second, even)
-    for load in loads[1:4]:
-        load.wait()
+    with jax.named_scope("c_loads"):
+        for load in loads[:4]:
+            load.wait()
+    with jax.named_scope("e_kv"):
+        cosine, sine = rotary(order, frequency, first, second, even)
+        for h in range(HEADS):
+            cols = slice(h * HD, (h + 1) * HD)
+            k = turn(normed(ik[:, cols].astype(jnp.float32), gains[1:2, :]), cosine, sine, even)
+            v = iv[:, cols].astype(jnp.float32)
+            kv_out[h] = jnp.concatenate([k, v], axis=0).astype(jnp.bfloat16)
+
+    with jax.named_scope("f_barrier"):
+        @pl.when(owner)
+        def _():
+            pl.semaphore_wait(barrier, HEADS - 1)
+
+        @pl.when(jnp.logical_not(owner))
+        def _():
+            pl.semaphore_wait(barrier, HEADS)
 
     for h in range(HEADS):
-        cols = slice(h * HD, (h + 1) * HD)
-        k = turn(normed(ik[:, cols].astype(jnp.float32), gains[1:2, :]), cosine, sine, even)
-        v = iv[:, cols].astype(jnp.float32)
-        kv_out[h] = jnp.concatenate([k, v], axis=0).astype(jnp.bfloat16)
-
-    @pl.when(owner)
-    def _():
-        pl.semaphore_wait(barrier, HEADS - 1)
-
-    @pl.when(jnp.logical_not(owner))
-    def _():
-        pl.semaphore_wait(barrier, HEADS)
-
-    for h in range(HEADS):
-        @pl.when(me != OWNERS[h])
+        @pl.when(me != owners[h])
         def _():
             pltpu.make_async_remote_copy(
                 src_ref=kv_out.at[h], dst_ref=kv_in.at[spot], send_sem=kv_send, recv_sem=kv_recv.at[z],
-                device_id={"seq": OWNERS[h]}, device_id_type=MESH).start()
+                device_id={"seq": owners[h]}, device_id_type=MESH).start()
 
     for load in loads[4:]:
         load.wait()
@@ -143,11 +162,11 @@
         q = turn(normed(iq[:, cols].astype(jnp.float32), gains[0:1, :]), cosine, sine, even)
         q_out[h] = q.astype(jnp.bfloat16)
     for h in range(HEADS):
-        @pl.when(me != OWNERS[h])
+        @pl.when(me != owners[h])
         def _():
             pltpu.make_async_remote_copy(
                 src_ref=q_out.at[h], dst_ref=q_in.at[spot], send_sem=q_send, recv_sem=q_recv.at[z],
-                device_id={"seq": OWNERS[h]}, device_id_type=MESH).start()
+                device_id={"seq": owners[h]}, device_id_type=MESH).start()
 
     def drain(ref, count, sem):
         pltpu.make_async_copy(ref.at[pl.ds(0, count)], ref.at[pl.ds(0, count)], sem).wait()
@@ -189,49 +208,58 @@
 
         early = {}
         for group in (0, 1):
-            arrived(q_in, q_recv, group)
-            q = queries(group)
-            early[group] = (q, text_part(q))
-        for group in range(4):
-            arrived(kv_in, kv_recv, group)
+            with jax.named_scope("k%d_q" % group):
+                arrived(q_in, q_recv, group)
+            with jax.named_scope("k%d_text" % group):
+                q = queries(group)
+                early[group] = (q, text_part(q))
+        for group in (0, 1, 3, 2):
+            with jax.named_scope("l%d_kv" % group):
+                arrived(kv_in, kv_recv, group)
         kv = kv_in[...].astype(jnp.float32)
         k = kv[:, :ROWS, :].reshape(SEQ * ROWS, HD).astype(jnp.bfloat16)
         v = kv[:, ROWS:, :].reshape(SEQ * ROWS, HD).astype(jnp.bfloat16)
         for group in (0, 1, 3, 2):
             if group not in early:
-                arrived(q_in, q_recv, group)
-                q = queries(group)
-                early[group] = (q, text_part(q))
-            q, (text_max, text_sum, text_out) = early[group]
-            s = scores_of(q, k)
-            top = jnp.maximum(jnp.max(s, axis=-1, keepdims=True), text_max)
-            e = jnp.exp2((s - top) * scale)
-            keep = jnp.exp2((text_max - top) * scale)
-            total = jnp.sum(e, axis=-1, keepdims=True) + text_sum * keep
-            o = jnp.dot(e.astype(jnp.bfloat16), v, preferred_element_type=jnp.float32) + text_out * keep
-            o = (o / total).astype(jnp.bfloat16)
-            o_out[pl.ds(group * PLANE, PLANE)] = o.reshape(PLANE, 2 * ROWS, HD)
-            for i in range(PLANE):
-                to = at(i // 4, group, i % 4)
-
-                def send():
-                    pltpu.make_async_remote_copy(
-                        src_ref=o_out.at[group * PLANE + i], dst_ref=o_in.at[head], send_sem=o_send,
-                        recv_sem=o_recv, device_id={"seq": to}, device_id_type=MESH).start()
-
-                if to in OWNERS:
-                    pl.when(me != to)(send)
-                else:
-                    send()
+                with jax.named_scope("n%d_q" % group):
+                    arrived(q_in, q_recv, group)
+                with jax.named_scope("n%d_text" % group):
+                    q = queries(group)
+                    early[group] = (q, text_part(q))
+            with jax.named_scope("n%d_image" % group):
+                q, (text_max, text_sum, text_out) = early[group]
+                s = scores_of(q, k)
+                top = jnp.maximum(jnp.max(s, axis=-1, keepdims=True), text_max)
+                e = jnp.exp2((s - top) * scale)
+                keep = jnp.exp2((text_max - top) * scale)
+                total = jnp.sum(e, axis=-1, keepdims=True) + text_sum * keep
+                o = jnp.dot(e.astype(jnp.bfloat16), v, preferred_element_type=jnp.float32) + text_out * keep
+                o = (o / total).astype(jnp.bfloat16)
+                o_out[pl.ds(group * PLANE, PLANE)] = o.reshape(PLANE, 2 * ROWS, HD)
+            with jax.named_scope("n%d_send" % group):
+                for i in range(PLANE):
+                    to = at(i // 4, group, i % 4)
+
+                    def send():
+                        pltpu.make_async_remote_copy(
+                            src_ref=o_out.at[group * PLANE + i], dst_ref=o_in.at[head], send_sem=o_send,
+                            recv_sem=o_recv, device_id={"seq": to}, device_id_type=MESH).start()
+
+                    if to in OWNING:
+                        pl.when(me != to)(send)
+                    else:
+                        send()
         o_in[head] = o_out[spot]
-        drain(o_in, HEADS - 1, o_recv)
+        with jax.named_scope("o_wait"):
+            drain(o_in, HEADS - 1, o_recv)
         drain(kv_out, HEADS - 1, kv_send)
         drain(q_out, HEADS - 1, q_send)
         drain(o_out, SEQ - 1, o_send)
 
     @pl.when(jnp.logical_not(owner))
     def _():
-        drain(o_in, HEADS, o_recv)
+        with jax.named_scope("p_wait"):
+            drain(o_in, HEADS, o_recv)
         drain(kv_out, HEADS, kv_send)
         drain(q_out, HEADS, q_send)
 

time: 23.2 us -> 20.3 us (0.88)
  Pallas kernels: 21.7 us -> 18.8 us
    pallas_call x1, Pallas kernels: 21.1 us -> 18.2 us  [local(): pl.pallas_call(kernel, out_shape=pltpu.VMEM((HEADS, 2 * ROWS, HD), bf16),...]
where the time goes in v3:
time: 20.3 us; the launch traced here: 20.1 us
  Pallas kernels  18.8 us (93%)
  between operations  1.29 us (6%)
    pallas_call x1, Pallas kernels, local(): pl.pallas_call(kernel, out_shape=pltpu.VMEM((HEADS, 2 * ROWS, HD), bf16),...  18.2 us
    pallas_call x1, Pallas kernels, local(): pl.pallas_call(spread, out_shape=(out, out), in_specs=[vmem], out_specs=(...  0.64 us

profile of v3, /device:TPU:4, one launch (start us, length us, event | category | flops | bytes accessed | tf_op | source)
XLA Modules:
  0.0 20.1 jit_solution(15459293581822219215)
XLA Ops:
  1.3 18.2 %joint.1.o_in = bf16[12,16,128]{2,1,0:T(8,128)(2,1)S(1)} custom-call(s32[8]{0:T(128)} %order_hbm.1, s32[1]{0:T(128)S(6)} %copy.14.length_ref, bf16[8,1536]{1,0:T(8,128)(2,1)} %iq_hbm.1, bf16[8,1536]{1,0:T(8,128)(2,1)} %ik_hbm.1, bf16[8,1536]{1,0:T(8,128)(2,1)} %iv_hbm.1, bf16[512,1536]{1,0:T(8,128)(2,1)} %tq_hbm.1, bf16[512,1536]{1,0:T(8,128)(2,1)} %tk_hbm.1, ...), custom_call_target="tpu_custom_call" | custom-call | tf_op jit(solution)/shard_map/joint/pallas_call | solution.py:290
  19.5 0.6 %spread.1 = (bf16[8,1536]{1,0:T(8,128)(2,1)}, bf16[8,1536]{1,0:T(8,128)(2,1)}) custom-call(bf16[12,16,128]{2,1,0:T(8,128)(2,1)S(1)} %joint.1.o_in), custom_call_target="tpu_custom_call" | custom-call | tf_op jit(solution)/shard_map/spread/pallas_call | solution.py:315

commit v4 on v3

--- a/solution.py
+++ b/solution.py
@@ -22,10 +22,10 @@
 
 
 OWNERS = (
-    [at(0, 0, 0), at(1, 0, 0), at(0, 0, 1), at(0, 1, 0), at(1, 0, 1), at(1, 1, 0),
-     at(0, 1, 1), at(2, 0, 0), at(0, 0, 2), at(0, 2, 0), at(1, 1, 1), at(3, 0, 0)],
-    [at(0, 0, 3), at(1, 0, 2), at(2, 0, 1), at(3, 0, 1), at(1, 0, 3), at(2, 0, 2),
-     at(2, 1, 0), at(0, 1, 2), at(3, 1, 0), at(0, 1, 3), at(1, 1, 2), at(2, 1, 1)],
+    [at(0, 0, 0), at(1, 0, 0), at(0, 0, 1), at(0, 1, 0), at(3, 0, 0), at(1, 0, 1),
+     at(0, 0, 2), at(2, 0, 0), at(1, 1, 0), at(2, 0, 1), at(0, 1, 1), at(0, 0, 3)],
+    [at(3, 0, 1), at(1, 0, 2), at(1, 0, 3), at(2, 1, 0), at(2, 0, 2), at(3, 1, 0),
+     at(0, 1, 2), at(1, 1, 1), at(0, 1, 3), at(2, 1, 1), at(1, 1, 2), at(3, 1, 1)],
 )
 OWNING = set(OWNERS[0] + OWNERS[1])
 
@@ -34,7 +34,7 @@
     return min(a, 4 - a)
 
 
-FAR_FIRST = sorted(range(SEQ), key=lambda t: -(ring(t // 16) + 1.5 * ring(t // 4 % 4) + ring(t % 4)))
+FAR_FIRST = sorted([(t // 16, t // 4 % 4, t % 4) for t in range(1, SEQ)], key=lambda d: -sum(map(ring, d)))
 
 
 def normed(x, gain):
@@ -75,10 +75,10 @@
     return lax.dot_general(q, k, (((1,), (1,)), ((), ())), preferred_element_type=jnp.float32)
 
 
-def kernel(order_hbm, length_ref, iq_hbm, ik_hbm, iv_hbm, tq_hbm, tk_hbm, tv_hbm,
+def kernel(order_hbm, length_hbm, iq_hbm, ik_hbm, iv_hbm, tq_hbm, tk_hbm, tv_hbm,
            iq_gain_hbm, ik_gain_hbm, tq_gain_hbm, tk_gain_hbm,
            o_in,
-           order, iq, ik, iv, tq, tk, tv, gains, kv_out, q_out, kv_in, q_in, o_out,
+           order, length, iq, ik, iv, tq, tk, tv, gains, kv_out, q_out, kv_in, q_in, o_out,
            load_sem, kv_send, kv_recv, q_send, q_recv, o_send, o_recv):
     me = lax.axis_index("seq")
     x, z, y = me // 16, (me // 4) % 4, me % 4
@@ -106,6 +106,7 @@
     barrier = pltpu.get_barrier_semaphore()
     column = pl.ds(pl.multiple_of(head * HD, HD), HD)
     text_loads = [
+        pltpu.make_async_copy(length_hbm, length, load_sem.at[11]),
         pltpu.make_async_copy(tk_gain_hbm, gains.at[3:4], load_sem.at[6]),
         pltpu.make_async_copy(tk_hbm.at[:, column], tk, load_sem.at[7]),
         pltpu.make_async_copy(tq_gain_hbm, gains.at[2:3], load_sem.at[8]),
@@ -116,14 +117,12 @@
     @pl.when(owner)
     def _():
         with jax.named_scope("b_greet"):
-            for t in FAR_FIRST:
-                def greet():
-                    pl.semaphore_signal(barrier, inc=1, device_id={"seq": t}, device_id_type=MESH)
-
-                if t in OWNING:
-                    pl.when(me != t)(greet)
-                else:
-                    greet()
+            xs = [(x + d) % 4 * 16 for d in range(4)]
+            zs = [(z + d) % 4 * 4 for d in range(4)]
+            ys = [(y + d) % 4 for d in range(4)]
+            for dx, dz, dy in FAR_FIRST:
+                pl.semaphore_signal(
+                    barrier, inc=1, device_id={"seq": xs[dx] + zs[dz] + ys[dy]}, device_id_type=MESH)
         for load in text_loads:
             load.start()
 
@@ -186,56 +185,73 @@
         q_in[spot] = q_out[head]
         for load in text_loads:
             load.wait()
-        text_keys = normed(tk[...].astype(jnp.float32), gains[3:4, :]).astype(jnp.bfloat16)
-        text_queries = normed(tq[...].astype(jnp.float32), gains[2:3, :])
-        text_values = tv[...]
-
-        def queries(group):
-            image = q_in[pl.ds(group * PLANE, PLANE)].astype(jnp.float32)
-            text = jnp.concatenate(
-                [text_queries[i * 128 + group * 32:i * 128 + group * 32 + 32] for i in range(4)], axis=0)
-            both = jnp.concatenate([image, text.reshape(PLANE, ROWS, HD)], axis=1)
-            return both.reshape(PLANE * 2 * ROWS, HD).astype(jnp.bfloat16)
-
-        def text_part(q):
-            s = scores_of(q, text_keys)
-            valid = lax.broadcasted_iota(jnp.int32, s.shape, 1) < length_ref[0]
-            s = jnp.where(valid, s, NEG)
-            top = jnp.max(s, axis=-1, keepdims=True)
-            e = jnp.exp2((s - top) * scale)
-            total = jnp.sum(e, axis=-1, keepdims=True)
-            return top, total, jnp.dot(e.astype(jnp.bfloat16), text_values, preferred_element_type=jnp.float32)
-
-        early = {}
-        for group in (0, 1):
-            with jax.named_scope("k%d_q" % group):
-                arrived(q_in, q_recv, group)
-            with jax.named_scope("k%d_text" % group):
-                q = queries(group)
-                early[group] = (q, text_part(q))
-        for group in (0, 1, 3, 2):
-            with jax.named_scope("l%d_kv" % group):
+        with jax.named_scope("j_text"):
+            text_keys = normed(tk[...].astype(jnp.float32), gains[3:4, :]).astype(jnp.bfloat16)
+            text_values = tv[...]
+            valid = lax.broadcasted_iota(jnp.int32, (1, text_keys.shape[0]), 1) < length[0]
+
+            def text_part(q):
+                s = jnp.where(valid, scores_of(q, text_keys), NEG)
+                top = jnp.max(s, axis=-1, keepdims=True)
+                e = jnp.exp2((s - top) * scale)
+                total = jnp.sum(e, axis=-1, keepdims=True)
+                return top, total, jnp.dot(e.astype(jnp.bfloat16), text_values, preferred_element_type=jnp.float32)
+
+            half = PLANE * ROWS
+            text_queries, text_state = {}, {}
+            for group in range(4):
+                rows = jnp.concatenate(
+                    [tq[pl.ds(i * half + group * 32, 32), :] for i in range(4)], axis=0).astype(jnp.float32)
+                text_queries[group] = normed(rows, gains[2:3, :]).astype(jnp.bfloat16)
+
+        def both_parts(first, second):
+            parts = text_part(jnp.concatenate([first, second], axis=0))
+            return tuple(part[:half] for part in parts), tuple(part[half:] for part in parts)
+
+        def image_queries(group):
+            return q_in[pl.ds(group * PLANE, PLANE)].astype(jnp.float32).reshape(half, HD).astype(jnp.bfloat16)
+
+        image_q, image_state = {}, {}
+        with jax.named_scope("j_part"):
+            for a, b in ((0, 1), (2, 3)):
+                text_state[a], text_state[b] = both_parts(text_queries[a], text_queries[b])
+
+        def image_part(a, b):
+            for group in (a, b):
+                image_q[group] = image_queries(group)
+            image_state[a], image_state[b] = both_parts(image_q[a], image_q[b])
+
+        with jax.named_scope("k_q"):
+            arrived(q_in, q_recv, 0)
+            arrived(q_in, q_recv, 1)
+        with jax.named_scope("k_text"):
+            image_part(0, 1)
+        with jax.named_scope("l_kv"):
+            for group in (0, 1, 3, 2):
                 arrived(kv_in, kv_recv, group)
         kv = kv_in[...].astype(jnp.float32)
         k = kv[:, :ROWS, :].reshape(SEQ * ROWS, HD).astype(jnp.bfloat16)
         v = kv[:, ROWS:, :].reshape(SEQ * ROWS, HD).astype(jnp.bfloat16)
-        for group in (0, 1, 3, 2):
-            if group not in early:
-                with jax.named_scope("n%d_q" % group):
-                    arrived(q_in, q_recv, group)
-                with jax.named_scope("n%d_text" % group):
-                    q = queries(group)
-                    early[group] = (q, text_part(q))
+        for group in (0, 1, 2, 3):
+            if group == 2:
+                with jax.named_scope("l_q"):
+                    arrived(q_in, q_recv, 2)
+                    arrived(q_in, q_recv, 3)
+                with jax.named_scope("m_text"):
+                    image_part(2, 3)
             with jax.named_scope("n%d_image" % group):
-                q, (text_max, text_sum, text_out) = early[group]
+                q = jnp.concatenate([image_q[group], text_queries[group]], axis=0)
+                text_max, text_sum, text_out = (
+                    jnp.concatenate(part, axis=0) for part in zip(image_state[group], text_state[group]))
                 s = scores_of(q, k)
                 top = jnp.maximum(jnp.max(s, axis=-1, keepdims=True), text_max)
                 e = jnp.exp2((s - top) * scale)
                 keep = jnp.exp2((text_max - top) * scale)
                 total = jnp.sum(e, axis=-1, keepdims=True) + text_sum * keep
                 o = jnp.dot(e.astype(jnp.bfloat16), v, preferred_element_type=jnp.float32) + text_out * keep
-                o = (o / total).astype(jnp.bfloat16)
-                o_out[pl.ds(group * PLANE, PLANE)] = o.reshape(PLANE, 2 * ROWS, HD)
+                o = o / total
+                image, text = o[:half].reshape(PLANE, ROWS, HD), o[half:].reshape(PLANE, ROWS, HD)
+                o_out[pl.ds(group * PLANE, PLANE)] = jnp.concatenate([image, text], axis=1).astype(jnp.bfloat16)
             with jax.named_scope("n%d_send" % group):
                 for i in range(PLANE):
                     to = at(i // 4, group, i % 4)
@@ -280,7 +296,6 @@
 def local(image_query, image_key, image_value, text_query, text_key, text_value, image_query_gain,
           image_key_gain, text_query_gain, text_key_gain, image_order, text_length):
     hbm = pl.BlockSpec(memory_space=pl.ANY)
-    smem = pl.BlockSpec(memory_space=pltpu.SMEM)
     vmem = pl.BlockSpec(memory_space=pltpu.VMEM)
     bf16, f32 = jnp.bfloat16, jnp.float32
     width = image_query.shape[1]
@@ -290,10 +305,11 @@
     blocks = pl.pallas_call(
         kernel,
         out_shape=pltpu.VMEM((HEADS, 2 * ROWS, HD), bf16),
-        in_specs=[hbm, smem] + [hbm] * 10,
+        in_specs=[hbm] * 12,
         out_specs=vmem,
         scratch_shapes=[
             pltpu.SMEM((ROWS,), jnp.int32),
+            pltpu.SMEM((1,), jnp.int32),
             pltpu.VMEM((ROWS, width), bf16),
             pltpu.VMEM((ROWS, width), bf16),
             pltpu.VMEM((ROWS, width), bf16),
@@ -306,7 +322,7 @@
             pltpu.VMEM((SEQ, 2 * ROWS, HD), bf16),
             pltpu.VMEM((SEQ, ROWS, HD), bf16),
             pltpu.VMEM((SEQ, 2 * ROWS, HD), bf16),
-            dma((11,)), dma, dma((4,)), dma, dma((4,)), dma, dma,
+            dma((12,)), dma, dma((4,)), dma, dma((4,)), dma, dma,
         ],
         compiler_params=pltpu.CompilerParams(collective_id=0, has_side_effects=True),
         name="joint",

time: 20.3 us -> 19.6 us (0.966)
  the two profiles are of different devices: /device:TPU:4 before, /device:TPU:1 now
where the time goes in v4:
time: 19.6 us; the launch traced here: 19.4 us
  Pallas kernels  18.2 us (93%)
  between operations  1.29 us (7%)
    pallas_call x1, Pallas kernels, local(): pl.pallas_call(kernel, out_shape=pltpu.VMEM((HEADS, 2 * ROWS, HD), bf16),...  17.5 us
    pallas_call x1, Pallas kernels, local(): pl.pallas_call(spread, out_shape=(out, out), in_specs=[vmem], out_specs=(...  0.64 us

profile of v4, /device:TPU:1, one launch (start us, length us, event | category | flops | bytes accessed | tf_op | source)
XLA Modules:
  0.0 19.4 jit_solution(10485482488758012994)
XLA Ops:
  1.3 17.5 %joint.1.o_in = bf16[12,16,128]{2,1,0:T(8,128)(2,1)S(1)} custom-call(s32[8]{0:T(128)} %order_hbm.1, s32[1]{0:T(128)S(6)} %copy.14.length_hbm, bf16[8,1536]{1,0:T(8,128)(2,1)} %iq_hbm.1, bf16[8,1536]{1,0:T(8,128)(2,1)} %ik_hbm.1, bf16[8,1536]{1,0:T(8,128)(2,1)} %iv_hbm.1, bf16[512,1536]{1,0:T(8,128)(2,1)} %tq_hbm.1, bf16[512,1536]{1,0:T(8,128)(2,1)} %tk_hbm.1, ...), custom_call_target="tpu_custom_call" | custom-call | tf_op jit(solution)/shard_map/joint/pallas_call | solution.py:305
  18.8 0.6 %spread.1 = (bf16[8,1536]{1,0:T(8,128)(2,1)}, bf16[8,1536]{1,0:T(8,128)(2,1)}) custom-call(bf16[12,16,128]{2,1,0:T(8,128)(2,1)S(1)} %joint.1.o_in), custom_call_target="tpu_custom_call" | custom-call | tf_op jit(solution)/shard_map/spread/pallas_call | solution.py:331

commit v5 on v4

--- a/solution.py
+++ b/solution.py
@@ -71,14 +71,22 @@
     return x * cosine + other * sine
 
 
-def scores_of(q, k):
-    return lax.dot_general(q, k, (((1,), (1,)), ((), ())), preferred_element_type=jnp.float32)
+def wide(column):
+    return jnp.broadcast_to(column, (column.shape[0], HD))
+
+
+def across(block, like):
+    return jnp.concatenate([block] * (like.shape[1] // HD), axis=1)
+
+
+def dot(a, b):
+    return jnp.dot(a, b, preferred_element_type=jnp.float32)
 
 
 def kernel(order_hbm, length_hbm, iq_hbm, ik_hbm, iv_hbm, tq_hbm, tk_hbm, tv_hbm,
            iq_gain_hbm, ik_gain_hbm, tq_gain_hbm, tk_gain_hbm,
            o_in,
-           order, length, iq, ik, iv, tq, tk, tv, gains, kv_out, q_out, kv_in, q_in, o_out,
+           order, length, iq, ik, iv, tq, tk, tv, gains, kv_out, q_out, kv_in, q_in, keys, values, o_out,
            load_sem, kv_send, kv_recv, q_send, q_recv, o_send, o_recv):
     me = lax.axis_index("seq")
     x, z, y = me // 16, (me // 4) % 4, me % 4
@@ -186,16 +194,16 @@
         for load in text_loads:
             load.wait()
         with jax.named_scope("j_text"):
-            text_keys = normed(tk[...].astype(jnp.float32), gains[3:4, :]).astype(jnp.bfloat16)
+            text_keys = normed(tk[...].astype(jnp.float32), gains[3:4, :]).T.astype(jnp.bfloat16)
             text_values = tv[...]
-            valid = lax.broadcasted_iota(jnp.int32, (1, text_keys.shape[0]), 1) < length[0]
+            valid = lax.broadcasted_iota(jnp.int32, (1, text_keys.shape[1]), 1) < length[0]
 
             def text_part(q):
-                s = jnp.where(valid, scores_of(q, text_keys), NEG)
-                top = jnp.max(s, axis=-1, keepdims=True)
-                e = jnp.exp2((s - top) * scale)
-                total = jnp.sum(e, axis=-1, keepdims=True)
-                return top, total, jnp.dot(e.astype(jnp.bfloat16), text_values, preferred_element_type=jnp.float32)
+                s = jnp.where(valid, dot(q, text_keys), NEG)
+                top = wide(jnp.max(s, axis=-1, keepdims=True))
+                e = jnp.exp2((s - across(top, s)) * scale)
+                total = wide(jnp.sum(e, axis=-1, keepdims=True))
+                return top, total, dot(e.astype(jnp.bfloat16), text_values)
 
             half = PLANE * ROWS
             text_queries, text_state = {}, {}
@@ -220,6 +228,13 @@
             for group in (a, b):
                 image_q[group] = image_queries(group)
             image_state[a], image_state[b] = both_parts(image_q[a], image_q[b])
+
+        def take_keys(group):
+            arrived(kv_in, kv_recv, group)
+            kv = kv_in[pl.ds(group * PLANE, PLANE)].astype(jnp.float32)
+            rows = pl.ds(group * half, half)
+            keys[:, rows] = kv[:, :ROWS, :].reshape(half, HD).T.astype(jnp.bfloat16)
+            values[rows, :] = kv[:, ROWS:, :].reshape(half, HD).astype(jnp.bfloat16)
 
         with jax.named_scope("k_q"):
             arrived(q_in, q_recv, 0)
@@ -228,10 +243,7 @@
             image_part(0, 1)
         with jax.named_scope("l_kv"):
             for group in (0, 1, 3, 2):
-                arrived(kv_in, kv_recv, group)
-        kv = kv_in[...].astype(jnp.float32)
-        k = kv[:, :ROWS, :].reshape(SEQ * ROWS, HD).astype(jnp.bfloat16)
-        v = kv[:, ROWS:, :].reshape(SEQ * ROWS, HD).astype(jnp.bfloat16)
+                take_keys(group)
         for group in (0, 1, 2, 3):
             if group == 2:
                 with jax.named_scope("l_q"):
@@ -243,12 +255,12 @@
                 q = jnp.concatenate([image_q[group], text_queries[group]], axis=0)
                 text_max, text_sum, text_out = (
                     jnp.concatenate(part, axis=0) for part in zip(image_state[group], text_state[group]))
-                s = scores_of(q, k)
-                top = jnp.maximum(jnp.max(s, axis=-1, keepdims=True), text_max)
-                e = jnp.exp2((s - top) * scale)
+                s = dot(q, keys[...])
+                top = jnp.maximum(wide(jnp.max(s, axis=-1, keepdims=True)), text_max)
+                e = jnp.exp2((s - across(top, s)) * scale)
                 keep = jnp.exp2((text_max - top) * scale)
-                total = jnp.sum(e, axis=-1, keepdims=True) + text_sum * keep
-                o = jnp.dot(e.astype(jnp.bfloat16), v, preferred_element_type=jnp.float32) + text_out * keep
+                total = wide(jnp.sum(e, axis=-1, keepdims=True)) + text_sum * keep
+                o = dot(e.astype(jnp.bfloat16), values[...]) + text_out * keep
                 o = o / total
                 image, text = o[:half].reshape(PLANE, ROWS, HD), o[half:].reshape(PLANE, ROWS, HD)
                 o_out[pl.ds(group * PLANE, PLANE)] = jnp.concatenate([image, text], axis=1).astype(jnp.bfloat16)
@@ -321,6 +333,8 @@
             pltpu.VMEM((HEADS, ROWS, HD), bf16),
             pltpu.VMEM((SEQ, 2 * ROWS, HD), bf16),
             pltpu.VMEM((SEQ, ROWS, HD), bf16),
+            pltpu.VMEM((HD, SEQ * ROWS), bf16),
+            pltpu.VMEM((SEQ * ROWS, HD), bf16),
             pltpu.VMEM((SEQ, 2 * ROWS, HD), bf16),
             dma((12,)), dma, dma((4,)), dma, dma((4,)), dma, dma,
         ],

time: 19.6 us -> 19.4 us (0.990)
  Pallas kernels: 18.2 us -> 17.9 us
    pallas_call x1, Pallas kernels: 17.5 us -> 17.3 us  [local(): pl.pallas_call(kernel, out_shape=pltpu.VMEM((HEADS, 2 * ROWS, HD), bf16),...]
where the time goes in v5:
time: 19.4 us; the launch traced here: 19.2 us
  Pallas kernels  17.9 us (92%)
  between operations  1.29 us (7%)
    pallas_call x1, Pallas kernels, local(): pl.pallas_call(kernel, out_shape=pltpu.VMEM((HEADS, 2 * ROWS, HD), bf16),...  17.3 us
    pallas_call x1, Pallas kernels, local(): pl.pallas_call(spread, out_shape=(out, out), in_specs=[vmem], out_specs=(...  0.64 us

profile of v5, /device:TPU:1, one launch (start us, length us, event | category | flops | bytes accessed | tf_op | source)
XLA Modules:
  0.0 19.2 jit_solution(13763450396540578174)
XLA Ops:
  1.3 17.3 %joint.1.o_in = bf16[12,16,128]{2,1,0:T(8,128)(2,1)S(1)} custom-call(s32[8]{0:T(128)} %order_hbm.1, s32[1]{0:T(128)S(6)} %copy.14.length_hbm, bf16[8,1536]{1,0:T(8,128)(2,1)} %iq_hbm.1, bf16[8,1536]{1,0:T(8,128)(2,1)} %ik_hbm.1, bf16[8,1536]{1,0:T(8,128)(2,1)} %iv_hbm.1, bf16[512,1536]{1,0:T(8,128)(2,1)} %tq_hbm.1, bf16[512,1536]{1,0:T(8,128)(2,1)} %tk_hbm.1, ...), custom_call_target="tpu_custom_call" | custom-call | tf_op jit(solution)/shard_map/joint/pallas_call | solution.py:317
  18.6 0.6 %spread.1 = (bf16[8,1536]{1,0:T(8,128)(2,1)}, bf16[8,1536]{1,0:T(8,128)(2,1)}) custom-call(bf16[12,16,128]{2,1,0:T(8,128)(2,1)S(1)} %joint.1.o_in), custom_call_target="tpu_custom_call" | custom-call | tf_op jit(solution)/shard_map/spread/pallas_call | solution.py:345

commit v6 on v5

--- a/solution.py
+++ b/solution.py
@@ -27,7 +27,7 @@
     [at(3, 0, 1), at(1, 0, 2), at(1, 0, 3), at(2, 1, 0), at(2, 0, 2), at(3, 1, 0),
      at(0, 1, 2), at(1, 1, 1), at(0, 1, 3), at(2, 1, 1), at(1, 1, 2), at(3, 1, 1)],
 )
-OWNING = set(OWNERS[0] + OWNERS[1])
+HOME = set(OWNERS[1])
 
 
 def ring(a):
@@ -66,9 +66,15 @@
     return jnp.cos(angle), jnp.where(even, -sine, sine)
 
 
-def turn(x, cosine, sine, even):
-    other = jnp.where(even, pltpu.roll(x, HD - 1, 1), pltpu.roll(x, 1, 1))
-    return x * cosine + other * sine
+def swap(x, even):
+    return jnp.where(even, pltpu.roll(x, HD - 1, 1), pltpu.roll(x, 1, 1))
+
+
+def turn(x, gain, cosine, sine, even):
+    gains = jnp.broadcast_to(gain, x.shape)
+    same, other = gains * cosine, swap(gains, even) * sine
+    scale = lax.rsqrt(jnp.mean(x * x, axis=-1, keepdims=True) + EPS)
+    return (x * same + swap(x, even) * other) * scale
 
 
 def wide(column):
@@ -86,21 +92,8 @@
 def kernel(order_hbm, length_hbm, iq_hbm, ik_hbm, iv_hbm, tq_hbm, tk_hbm, tv_hbm,
            iq_gain_hbm, ik_gain_hbm, tq_gain_hbm, tk_gain_hbm,
            o_in,
-           order, length, iq, ik, iv, tq, tk, tv, gains, kv_out, q_out, kv_in, q_in, keys, values, o_out,
-           load_sem, kv_send, kv_recv, q_send, q_recv, o_send, o_recv):
-    me = lax.axis_index("seq")
-    x, z, y = me // 16, (me // 4) % 4, me % 4
-    spot = z * 16 + x * 4 + y
-    other_request = lax.axis_index("req") == 1
-    owners = [jnp.where(other_request, b, a) for a, b in zip(*OWNERS)]
-    head = jnp.int32(0)
-    owner = me == owners[0]
-    for h in range(1, HEADS):
-        mine = me == owners[h]
-        head = jnp.where(mine, h, head)
-        owner = jnp.logical_or(owner, mine)
-    scale = HD ** -0.5 * LOG2E
-
+           order, length, iq, ik, iv, tq, tk, tv, gains, kv_out, q_out, kv_in, q_in, keys, values, o_out, length_out, length_in,
+           feed_send, feed_recv, load_sem, kv_send, kv_recv, q_send, q_recv, o_send, o_recv):
     loads = [
         pltpu.make_async_copy(order_hbm, order, load_sem.at[0]),
         pltpu.make_async_copy(ik_hbm, ik, load_sem.at[1]),
@@ -111,13 +104,33 @@
     ]
     for load in loads:
         load.start()
+    me, request = lax.axis_index("seq"), lax.axis_index("req")
+    x, z, y = me // 16, (me // 4) % 4, me % 4
+    spot = z * 16 + x * 4 + y
+    owners = [jnp.where(request == 1, b, a) for a, b in zip(*OWNERS)]
+    head = jnp.int32(0)
+    chip_first = me == OWNERS[0][0]
+    chip_second = me == OWNERS[1][0]
+    for h in range(1, HEADS):
+        first, second = me == OWNERS[0][h], me == OWNERS[1][h]
+        head = jnp.where(jnp.logical_or(first, second), h, head)
+        chip_first, chip_second = jnp.logical_or(chip_first, first), jnp.logical_or(chip_second, second)
+    feeder = jnp.logical_and(request == 0, chip_first)
+    guest = jnp.logical_and(request == 1, chip_first)
+    home = jnp.logical_and(request == 1, chip_second)
+    owner = jnp.logical_or(guest, home)
+    served = jnp.where(guest, 0, 1)
+    scale = HD ** -0.5 * LOG2E
+
     barrier = pltpu.get_barrier_semaphore()
     column = pl.ds(pl.multiple_of(head * HD, HD), HD)
+    length_load = pltpu.make_async_copy(length_hbm, length, load_sem.at[11])
+    gain_loads = [
+        pltpu.make_async_copy(tk_gain_hbm, gains.at[3:4], load_sem.at[6]),
+        pltpu.make_async_copy(tq_gain_hbm, gains.at[2:3], load_sem.at[8]),
+    ]
     text_loads = [
-        pltpu.make_async_copy(length_hbm, length, load_sem.at[11]),
-        pltpu.make_async_copy(tk_gain_hbm, gains.at[3:4], load_sem.at[6]),
         pltpu.make_async_copy(tk_hbm.at[:, column], tk, load_sem.at[7]),
-        pltpu.make_async_copy(tq_gain_hbm, gains.at[2:3], load_sem.at[8]),
         pltpu.make_async_copy(tq_hbm.at[:, column], tq, load_sem.at[9]),
         pltpu.make_async_copy(tv_hbm.at[:, column], tv, load_sem.at[10]),
     ]
@@ -130,9 +143,24 @@
             ys = [(y + d) % 4 for d in range(4)]
             for dx, dz, dy in FAR_FIRST:
                 pl.semaphore_signal(
-                    barrier, inc=1, device_id={"seq": xs[dx] + zs[dz] + ys[dy]}, device_id_type=MESH)
+                    barrier, inc=1, device_id={"req": served, "seq": xs[dx] + zs[dz] + ys[dy]}, device_id_type=MESH)
+
+            @pl.when(guest)
+            def _():
+                pl.semaphore_signal(barrier, inc=1, device_id={"req": 0, "seq": me}, device_id_type=MESH)
+
+        for load in gain_loads:
+            load.start()
+
+    @pl.when(home)
+    def _():
+        length_load.start()
         for load in text_loads:
             load.start()
+
+    @pl.when(feeder)
+    def _():
+        length_load.start()
 
     frequency, first, second, even = lanes()
     with jax.named_scope("c_loads"):
@@ -142,61 +170,94 @@
         cosine, sine = rotary(order, frequency, first, second, even)
         for h in range(HEADS):
             cols = slice(h * HD, (h + 1) * HD)
-            k = turn(normed(ik[:, cols].astype(jnp.float32), gains[1:2, :]), cosine, sine, even)
+            k = turn(ik[:, cols].astype(jnp.float32), gains[1:2, :], cosine, sine, even)
             v = iv[:, cols].astype(jnp.float32)
             kv_out[h] = jnp.concatenate([k, v], axis=0).astype(jnp.bfloat16)
 
     with jax.named_scope("f_barrier"):
-        @pl.when(owner)
+        @pl.when(home)
         def _():
             pl.semaphore_wait(barrier, HEADS - 1)
 
-        @pl.when(jnp.logical_not(owner))
+        @pl.when(jnp.logical_not(home))
         def _():
             pl.semaphore_wait(barrier, HEADS)
 
     for h in range(HEADS):
-        @pl.when(me != owners[h])
+        @pl.when(jnp.logical_or(request == 0, me != owners[h]))
         def _():
             pltpu.make_async_remote_copy(
                 src_ref=kv_out.at[h], dst_ref=kv_in.at[spot], send_sem=kv_send, recv_sem=kv_recv.at[z],
-                device_id={"seq": owners[h]}, device_id_type=MESH).start()
+                device_id={"req": 1, "seq": owners[h]}, device_id_type=MESH).start()
 
     for load in loads[4:]:
         load.wait()
     for h in range(HEADS):
         cols = slice(h * HD, (h + 1) * HD)
-        q = turn(normed(iq[:, cols].astype(jnp.float32), gains[0:1, :]), cosine, sine, even)
+        q = turn(iq[:, cols].astype(jnp.float32), gains[0:1, :], cosine, sine, even)
         q_out[h] = q.astype(jnp.bfloat16)
     for h in range(HEADS):
-        @pl.when(me != owners[h])
+        @pl.when(jnp.logical_or(request == 0, me != owners[h]))
         def _():
             pltpu.make_async_remote_copy(
                 src_ref=q_out.at[h], dst_ref=q_in.at[spot], send_sem=q_send, recv_sem=q_recv.at[z],
-                device_id={"seq": owners[h]}, device_id_type=MESH).start()
+                device_id={"req": 1, "seq": owners[h]}, device_id_type=MESH).start()
+
+    def feed(i, source, target):
+        return pltpu.make_async_remote_copy(
+            src_ref=source, dst_ref=target, send_sem=feed_send.at[i], recv_sem=feed_recv.at[i],
+            device_id={"req": 1, "seq": me}, device_id_type=MESH)
+
+    feeds = [
+        feed(0, tk_hbm.at[:, column], tk), feed(1, tq_hbm.at[:, column], tq), feed(2, tv_hbm.at[:, column], tv),
+        feed(3, length_out, length_in)]
+
+    @pl.when(feeder)
+    def _():
+        for copy in feeds[:3]:
+            copy.start()
+        length_load.wait()
+        length_out[...] = jnp.full(length_out.shape, length[0], jnp.int32)
+        feeds[3].start()
 
     def drain(ref, count, sem):
         pltpu.make_async_copy(ref.at[pl.ds(0, count)], ref.at[pl.ds(0, count)], sem).wait()
 
     def arrived(ref, sem, group):
-        @pl.when(z == group)
+        own = jnp.logical_and(home, z == group)
+
+        @pl.when(own)
         def _():
             drain(ref, PLANE - 1, sem.at[group])
 
-        @pl.when(z != group)
+        @pl.when(jnp.logical_not(own))
         def _():
             drain(ref, PLANE, sem.at[group])
 
     @pl.when(owner)
     def _():
-        kv_in[spot] = kv_out[head]
-        q_in[spot] = q_out[head]
-        for load in text_loads:
+        @pl.when(home)
+        def _():
+            kv_in[spot] = kv_out[head]
+            q_in[spot] = q_out[head]
+            length_load.wait()
+            length_in[...] = jnp.full(length_in.shape, length[0], jnp.int32)
+            for load in text_loads:
+                load.wait()
+
+        with jax.named_scope("j_feed"):
+            @pl.when(guest)
+            def _():
+                for copy in feeds:
+                    copy.wait_recv()
+
+        for load in gain_loads:
             load.wait()
         with jax.named_scope("j_text"):
             text_keys = normed(tk[...].astype(jnp.float32), gains[3:4, :]).T.astype(jnp.bfloat16)
             text_values = tv[...]
-            valid = lax.broadcasted_iota(jnp.int32, (1, text_keys.shape[1]), 1) < length[0]
+            keys_in = lax.broadcasted_iota(jnp.int32, (1, text_keys.shape[1]), 1)
+            valid = keys_in < across(length_in[0:1, :], keys_in)
 
             def text_part(q):
                 s = jnp.where(valid, dot(q, text_keys), NEG)
@@ -242,7 +303,7 @@
         with jax.named_scope("k_text"):
             image_part(0, 1)
         with jax.named_scope("l_kv"):
-            for group in (0, 1, 3, 2):
+            for group in (0, 1, 2, 3):
                 take_keys(group)
         for group in (0, 1, 2, 3):
             if group == 2:
@@ -271,25 +332,39 @@
                     def send():
                         pltpu.make_async_remote_copy(
                             src_ref=o_out.at[group * PLANE + i], dst_ref=o_in.at[head], send_sem=o_send,
-                            recv_sem=o_recv, device_id={"seq": to}, device_id_type=MESH).start()
-
-                    if to in OWNING:
-                        pl.when(me != to)(send)
+                            recv_sem=o_recv, device_id={"req": served, "seq": to}, device_id_type=MESH).start()
+
+                    if to in HOME:
+                        pl.when(jnp.logical_or(guest, me != to))(send)
                     else:
                         send()
-        o_in[head] = o_out[spot]
+        @pl.when(home)
+        def _():
+            o_in[head] = o_out[spot]
+            drain(o_out, SEQ - 1, o_send)
+
+        @pl.when(guest)
+        def _():
+            drain(o_out, SEQ, o_send)
+
+    @pl.when(feeder)
+    def _():
+        for copy in feeds:
+            copy.wait_send()
+
+    @pl.when(home)
+    def _():
+        drain(kv_out, HEADS - 1, kv_send)
+        drain(q_out, HEADS - 1, q_send)
         with jax.named_scope("o_wait"):
             drain(o_in, HEADS - 1, o_recv)
-        drain(kv_out, HEADS - 1, kv_send)
-        drain(q_out, HEADS - 1, q_send)
-        drain(o_out, SEQ - 1, o_send)
-
-    @pl.when(jnp.logical_not(owner))
-    def _():
+
+    @pl.when(jnp.logical_not(home))
+    def _():
+        drain(kv_out, HEADS, kv_send)
+        drain(q_out, HEADS, q_send)
         with jax.named_scope("p_wait"):
             drain(o_in, HEADS, o_recv)
-        drain(kv_out, HEADS, kv_send)
-        drain(q_out, HEADS, q_send)
 
 
 def spread(o_in, image_hbm, text_hbm, image, text, sem):
@@ -336,7 +411,9 @@
             pltpu.VMEM((HD, SEQ * ROWS), bf16),
             pltpu.VMEM((SEQ * ROWS, HD), bf16),
             pltpu.VMEM((SEQ, 2 * ROWS, HD), bf16),
-            dma((12,)), dma, dma((4,)), dma, dma((4,)), dma, dma,
+            pltpu.VMEM((ROWS, HD), jnp.int32),
+            pltpu.VMEM((ROWS, HD), jnp.int32),
+            dma((4,)), dma((4,)), dma((12,)), dma, dma((4,)), dma, dma((4,)), dma, dma,
         ],
         compiler_params=pltpu.CompilerParams(collective_id=0, has_side_effects=True),
         name="joint",

time: 19.4 us -> 19.4 us (level)
  no operation moved by 1% of the time
where the time goes in v6:
time: 19.4 us; the launch traced here: 19.2 us
  Pallas kernels  17.9 us (92%)
  between operations  1.29 us (7%)
    pallas_call x1, Pallas kernels, local(): pl.pallas_call(kernel, out_shape=pltpu.VMEM((HEADS, 2 * ROWS, HD), bf16),...  17.3 us
    pallas_call x1, Pallas kernels, local(): pl.pallas_call(spread, out_shape=(out, out), in_specs=[vmem], out_specs=(...  0.64 us

profile of v6, /device:TPU:1, one launch (start us, length us, event | category | flops | bytes accessed | tf_op | source)
XLA Modules:
  0.0 19.2 jit_solution(5151502439235984812)
XLA Ops:
  1.3 17.3 %joint.1.o_in = bf16[12,16,128]{2,1,0:T(8,128)(2,1)S(1)} custom-call(s32[8]{0:T(128)} %order_hbm.1, s32[1]{0:T(128)S(6)} %copy.14.length_hbm, bf16[8,1536]{1,0:T(8,128)(2,1)} %iq_hbm.1, bf16[8,1536]{1,0:T(8,128)(2,1)} %ik_hbm.1, bf16[8,1536]{1,0:T(8,128)(2,1)} %iv_hbm.1, bf16[512,1536]{1,0:T(8,128)(2,1)} %tq_hbm.1, bf16[512,1536]{1,0:T(8,128)(2,1)} %tk_hbm.1, ...), custom_call_target="tpu_custom_call" | custom-call | tf_op jit(solution)/shard_map/joint/pallas_call | solution.py:392
  18.6 0.6 %spread.1 = (bf16[8,1536]{1,0:T(8,128)(2,1)}, bf16[8,1536]{1,0:T(8,128)(2,1)}) custom-call(bf16[12,16,128]{2,1,0:T(8,128)(2,1)S(1)} %joint.1.o_in), custom_call_target="tpu_custom_call" | custom-call | tf_op jit(solution)/shard_map/spread/pallas_call | solution.py:422

commit v7 on v6

--- a/solution.py
+++ b/solution.py
@@ -25,7 +25,7 @@
     [at(0, 0, 0), at(1, 0, 0), at(0, 0, 1), at(0, 1, 0), at(3, 0, 0), at(1, 0, 1),
      at(0, 0, 2), at(2, 0, 0), at(1, 1, 0), at(2, 0, 1), at(0, 1, 1), at(0, 0, 3)],
     [at(3, 0, 1), at(1, 0, 2), at(1, 0, 3), at(2, 1, 0), at(2, 0, 2), at(3, 1, 0),
-     at(0, 1, 2), at(1, 1, 1), at(0, 1, 3), at(2, 1, 1), at(1, 1, 2), at(3, 1, 1)],
+     at(0, 1, 2), at(1, 1, 1), at(0, 1, 3), at(2, 0, 3), at(1, 1, 2), at(0, 3, 0)],
 )
 HOME = set(OWNERS[1])
 
@@ -92,16 +92,15 @@
 def kernel(order_hbm, length_hbm, iq_hbm, ik_hbm, iv_hbm, tq_hbm, tk_hbm, tv_hbm,
            iq_gain_hbm, ik_gain_hbm, tq_gain_hbm, tk_gain_hbm,
            o_in,
-           order, length, iq, ik, iv, tq, tk, tv, gains, kv_out, q_out, kv_in, q_in, keys, values, o_out, length_out, length_in,
-           feed_send, feed_recv, load_sem, kv_send, kv_recv, q_send, q_recv, o_send, o_recv):
-    loads = [
-        pltpu.make_async_copy(order_hbm, order, load_sem.at[0]),
-        pltpu.make_async_copy(ik_hbm, ik, load_sem.at[1]),
-        pltpu.make_async_copy(ik_gain_hbm, gains.at[1:2], load_sem.at[2]),
-        pltpu.make_async_copy(iv_hbm, iv, load_sem.at[3]),
-        pltpu.make_async_copy(iq_hbm, iq, load_sem.at[4]),
-        pltpu.make_async_copy(iq_gain_hbm, gains.at[0:1], load_sem.at[5]),
-    ]
+           order, length, rows_in, text_in, gains, kv_out, q_out, kv_in, q_in, keys, values, o_out, length_out, length_in,
+           order_sem, rows_sem, gain_sem, text_sem, length_sem, send_sem, kv_recv, q_recv, o_send, o_recv):
+    ik, iv, iq = rows_in.at[0], rows_in.at[1], rows_in.at[2]
+    tk, tv, tq = text_in.at[0], text_in.at[1], text_in.at[2]
+    loads = [pltpu.make_async_copy(order_hbm, order, order_sem)]
+    loads += [pltpu.make_async_copy(a, b, rows_sem) for a, b in ((ik_hbm, ik), (iv_hbm, iv), (iq_hbm, iq))]
+    loads += [
+        pltpu.make_async_copy(a, gains.at[i:i + 1], gain_sem)
+        for i, a in enumerate((iq_gain_hbm, ik_gain_hbm, tq_gain_hbm, tk_gain_hbm))]
     for load in loads:
         load.start()
     me, request = lax.axis_index("seq"), lax.axis_index("req")
@@ -124,16 +123,8 @@
 
     barrier = pltpu.get_barrier_semaphore()
     column = pl.ds(pl.multiple_of(head * HD, HD), HD)
-    length_load = pltpu.make_async_copy(length_hbm, length, load_sem.at[11])
-    gain_loads = [
-        pltpu.make_async_copy(tk_gain_hbm, gains.at[3:4], load_sem.at[6]),
-        pltpu.make_async_copy(tq_gain_hbm, gains.at[2:3], load_sem.at[8]),
-    ]
-    text_loads = [
-        pltpu.make_async_copy(tk_hbm.at[:, column], tk, load_sem.at[7]),
-        pltpu.make_async_copy(tq_hbm.at[:, column], tq, load_sem.at[9]),
-        pltpu.make_async_copy(tv_hbm.at[:, column], tv, load_sem.at[10]),
-    ]
+    length_load = pltpu.make_async_copy(length_hbm, length, length_sem)
+    text_slices = [(tk_hbm.at[:, column], tk), (tv_hbm.at[:, column], tv), (tq_hbm.at[:, column], tq)]
 
     @pl.when(owner)
     def _():
@@ -149,23 +140,24 @@
             def _():
                 pl.semaphore_signal(barrier, inc=1, device_id={"req": 0, "seq": me}, device_id_type=MESH)
 
-        for load in gain_loads:
-            load.start()
-
     @pl.when(home)
     def _():
         length_load.start()
-        for load in text_loads:
-            load.start()
+        for source, target in text_slices:
+            pltpu.make_async_copy(source, target, text_sem).start()
 
     @pl.when(feeder)
     def _():
         length_load.start()
 
     frequency, first, second, even = lanes()
+    def settle(ref, sem):
+        pltpu.make_async_copy(ref, ref, sem).wait()
+
     with jax.named_scope("c_loads"):
-        for load in loads[:4]:
-            load.wait()
+        loads[0].wait()
+        settle(gains, gain_sem)
+        settle(rows_in, rows_sem)
     with jax.named_scope("e_kv"):
         cosine, sine = rotary(order, frequency, first, second, even)
         for h in range(HEADS):
@@ -187,11 +179,9 @@
         @pl.when(jnp.logical_or(request == 0, me != owners[h]))
         def _():
             pltpu.make_async_remote_copy(
-                src_ref=kv_out.at[h], dst_ref=kv_in.at[spot], send_sem=kv_send, recv_sem=kv_recv.at[z],
+                src_ref=kv_out.at[h], dst_ref=kv_in.at[spot], send_sem=send_sem, recv_sem=kv_recv,
                 device_id={"req": 1, "seq": owners[h]}, device_id_type=MESH).start()
 
-    for load in loads[4:]:
-        load.wait()
     for h in range(HEADS):
         cols = slice(h * HD, (h + 1) * HD)
         q = turn(iq[:, cols].astype(jnp.float32), gains[0:1, :], cosine, sine, even)
@@ -200,39 +190,36 @@
         @pl.when(jnp.logical_or(request == 0, me != owners[h]))
         def _():
             pltpu.make_async_remote_copy(
-                src_ref=q_out.at[h], dst_ref=q_in.at[spot], send_sem=q_send, recv_sem=q_recv.at[z],
+                src_ref=q_out.at[h], dst_ref=q_in.at[spot], send_sem=send_sem, recv_sem=q_recv.at[z // 2],
                 device_id={"req": 1, "seq": owners[h]}, device_id_type=MESH).start()
 
-    def feed(i, source, target):
+    def feed(source, target, sem):
         return pltpu.make_async_remote_copy(
-            src_ref=source, dst_ref=target, send_sem=feed_send.at[i], recv_sem=feed_recv.at[i],
-            device_id={"req": 1, "seq": me}, device_id_type=MESH)
-
-    feeds = [
-        feed(0, tk_hbm.at[:, column], tk), feed(1, tq_hbm.at[:, column], tq), feed(2, tv_hbm.at[:, column], tv),
-        feed(3, length_out, length_in)]
+            src_ref=source, dst_ref=target, send_sem=sem, recv_sem=sem, device_id={"req": 1, "seq": me},
+            device_id_type=MESH)
 
     @pl.when(feeder)
     def _():
-        for copy in feeds[:3]:
-            copy.start()
+        for source, target in text_slices:
+            feed(source, target, text_sem).start()
         length_load.wait()
         length_out[...] = jnp.full(length_out.shape, length[0], jnp.int32)
-        feeds[3].start()
+        feed(length_out, length_in, length_sem).start()
 
     def drain(ref, count, sem):
-        pltpu.make_async_copy(ref.at[pl.ds(0, count)], ref.at[pl.ds(0, count)], sem).wait()
-
-    def arrived(ref, sem, group):
-        own = jnp.logical_and(home, z == group)
-
+        settle(ref.at[pl.ds(0, count)], sem)
+
+    def arrived(ref, count, sem, own):
         @pl.when(own)
         def _():
-            drain(ref, PLANE - 1, sem.at[group])
+            drain(ref, count - 1, sem)
 
         @pl.when(jnp.logical_not(own))
         def _():
-            drain(ref, PLANE, sem.at[group])
+            drain(ref, count, sem)
+
+    def queries_arrived(pair):
+        arrived(q_in, 2 * PLANE, q_recv.at[pair], jnp.logical_and(home, z // 2 == pair))
 
     @pl.when(owner)
     def _():
@@ -242,17 +229,14 @@
             q_in[spot] = q_out[head]
             length_load.wait()
             length_in[...] = jnp.full(length_in.shape, length[0], jnp.int32)
-            for load in text_loads:
-                load.wait()
 
         with jax.named_scope("j_feed"):
+            settle(text_in, text_sem)
+
             @pl.when(guest)
             def _():
-                for copy in feeds:
-                    copy.wait_recv()
-
-        for load in gain_loads:
-            load.wait()
+                settle(length_in, length_sem)
+
         with jax.named_scope("j_text"):
             text_keys = normed(tk[...].astype(jnp.float32), gains[3:4, :]).T.astype(jnp.bfloat16)
             text_values = tv[...]
@@ -290,33 +274,27 @@
                 image_q[group] = image_queries(group)
             image_state[a], image_state[b] = both_parts(image_q[a], image_q[b])
 
-        def take_keys(group):
-            arrived(kv_in, kv_recv, group)
-            kv = kv_in[pl.ds(group * PLANE, PLANE)].astype(jnp.float32)
-            rows = pl.ds(group * half, half)
-            keys[:, rows] = kv[:, :ROWS, :].reshape(half, HD).T.astype(jnp.bfloat16)
-            values[rows, :] = kv[:, ROWS:, :].reshape(half, HD).astype(jnp.bfloat16)
-
         with jax.named_scope("k_q"):
-            arrived(q_in, q_recv, 0)
-            arrived(q_in, q_recv, 1)
+            queries_arrived(0)
         with jax.named_scope("k_text"):
             image_part(0, 1)
         with jax.named_scope("l_kv"):
-            for group in (0, 1, 2, 3):
-                take_keys(group)
+            arrived(kv_in, SEQ, kv_recv, home)
+        kv = kv_in[...].astype(jnp.float32)
+        keys[...] = kv[:, :ROWS, :].reshape(SEQ * ROWS, HD).astype(jnp.bfloat16)
+        values[...] = kv[:, ROWS:, :].reshape(SEQ * ROWS, HD).astype(jnp.bfloat16)
         for group in (0, 1, 2, 3):
             if group == 2:
                 with jax.named_scope("l_q"):
-                    arrived(q_in, q_recv, 2)
-                    arrived(q_in, q_recv, 3)
+                    queries_arrived(1)
                 with jax.named_scope("m_text"):
                     image_part(2, 3)
             with jax.named_scope("n%d_image" % group):
                 q = jnp.concatenate([image_q[group], text_queries[group]], axis=0)
                 text_max, text_sum, text_out = (
                     jnp.concatenate(part, axis=0) for part in zip(image_state[group], text_state[group]))
-                s = dot(q, keys[...])
+                s = lax.dot_general(
+                    q, keys[...], (((1,), (1,)), ((), ())), preferred_element_type=jnp.float32)
                 top = jnp.maximum(wide(jnp.max(s, axis=-1, keepdims=True)), text_max)
                 e = jnp.exp2((s - across(top, s)) * scale)
                 keep = jnp.exp2((text_max - top) * scale)
@@ -349,20 +327,18 @@
 
     @pl.when(feeder)
     def _():
-        for copy in feeds:
-            copy.wait_send()
+        settle(text_in, text_sem)
+        settle(length_out, length_sem)
 
     @pl.when(home)
     def _():
-        drain(kv_out, HEADS - 1, kv_send)
-        drain(q_out, HEADS - 1, q_send)
+        drain(q_in, 3 * (HEADS - 1), send_sem)
         with jax.named_scope("o_wait"):
             drain(o_in, HEADS - 1, o_recv)
 
     @pl.when(jnp.logical_not(home))
     def _():
-        drain(kv_out, HEADS, kv_send)
-        drain(q_out, HEADS, q_send)
+        drain(q_in, 3 * HEADS, send_sem)
         with jax.named_scope("p_wait"):
             drain(o_in, HEADS, o_recv)
 
@@ -373,11 +349,9 @@
         cols = slice(h * HD, (h + 1) * HD)
         image[:, cols] = o[:ROWS].astype(jnp.bfloat16)
         text[:, cols] = o[ROWS:].astype(jnp.bfloat16)
-    stores = [pltpu.make_async_copy(image, image_hbm, sem.at[0]), pltpu.make_async_copy(text, text_hbm, sem.at[1])]
-    for store in stores:
-        store.start()
-    for store in stores:
-        store.wait()
+    pltpu.make_async_copy(image, image_hbm, sem).start()
+    pltpu.make_async_copy(text, text_hbm, sem).start()
+    pltpu.make_async_copy(o_in, o_in, sem).wait()
 
 
 def local(image_query, image_key, image_value, text_query, text_key, text_value, image_query_gain,
@@ -397,23 +371,19 @@
         scratch_shapes=[
             pltpu.SMEM((ROWS,), jnp.int32),
             pltpu.SMEM((1,), jnp.int32),
-            pltpu.VMEM((ROWS, width), bf16),
-            pltpu.VMEM((ROWS, width), bf16),
-            pltpu.VMEM((ROWS, width), bf16),
-            pltpu.VMEM((text_rows, HD), bf16),
-            pltpu.VMEM((text_rows, HD), bf16),
-            pltpu.VMEM((text_rows, HD), bf16),
+            pltpu.VMEM((3, ROWS, width), bf16),
+            pltpu.VMEM((3, text_rows, HD), bf16),
             pltpu.VMEM((4, HD), f32),
             pltpu.VMEM((HEADS, 2 * ROWS, HD), bf16),
             pltpu.VMEM((HEADS, ROWS, HD), bf16),
             pltpu.VMEM((SEQ, 2 * ROWS, HD), bf16),
             pltpu.VMEM((SEQ, ROWS, HD), bf16),
-            pltpu.VMEM((HD, SEQ * ROWS), bf16),
+            pltpu.VMEM((SEQ * ROWS, HD), bf16),
             pltpu.VMEM((SEQ * ROWS, HD), bf16),
             pltpu.VMEM((SEQ, 2 * ROWS, HD), bf16),
             pltpu.VMEM((ROWS, HD), jnp.int32),
             pltpu.VMEM((ROWS, HD), jnp.int32),
-            dma((4,)), dma((4,)), dma((12,)), dma, dma((4,)), dma, dma((4,)), dma, dma,
+            dma, dma, dma, dma, dma, dma, dma, dma((2,)), dma, dma,
         ],
         compiler_params=pltpu.CompilerParams(collective_id=0, has_side_effects=True),
         name="joint",
@@ -424,7 +394,7 @@
         out_shape=(out, out),
         in_specs=[vmem],
         out_specs=(hbm, hbm),
-        scratch_shapes=[pltpu.VMEM((ROWS, width), bf16), pltpu.VMEM((ROWS, width), bf16), dma((2,))],
+        scratch_shapes=[pltpu.VMEM((ROWS, width), bf16), pltpu.VMEM((ROWS, width), bf16), dma],
         name="spread",
     )(pltpu.with_memory_space_constraint(blocks, pltpu.VMEM))
 

time: 19.4 us -> 19.1 us (0.985)
  Pallas kernels: 17.9 us -> 17.6 us
    pallas_call x1, Pallas kernels: 17.3 us -> 17 us  [local(): pl.pallas_call(kernel, out_shape=pltpu.VMEM((HEADS, 2 * ROWS, HD), bf16),...]
where the time goes in v7:
time: 19.1 us; the launch traced here: 18.9 us
  Pallas kernels  17.6 us (92%)
  between operations  1.29 us (7%)
    pallas_call x1, Pallas kernels, local(): pl.pallas_call(kernel, out_shape=pltpu.VMEM((HEADS, 2 * ROWS, HD), bf16),...  17 us
    pallas_call x1, Pallas kernels, local(): pl.pallas_call(spread, out_shape=(out, out), in_specs=[vmem], out_specs=(...  0.63 us

profile of v7, /device:TPU:1, one launch (start us, length us, event | category | flops | bytes accessed | tf_op | source)
XLA Modules:
  0.0 18.9 jit_solution(12614373625204149752)
XLA Ops:
  1.3 17.0 %joint.1.o_in = bf16[12,16,128]{2,1,0:T(8,128)(2,1)S(1)} custom-call(s32[8]{0:T(128)} %order_hbm.1, s32[1]{0:T(128)S(6)} %copy.14.length_hbm, bf16[8,1536]{1,0:T(8,128)(2,1)} %iq_hbm.1, bf16[8,1536]{1,0:T(8,128)(2,1)} %ik_hbm.1, bf16[8,1536]{1,0:T(8,128)(2,1)} %iv_hbm.1, bf16[512,1536]{1,0:T(8,128)(2,1)} %tq_hbm.1, bf16[512,1536]{1,0:T(8,128)(2,1)} %tk_hbm.1, ...), custom_call_target="tpu_custom_call" | custom-call | tf_op jit(solution)/shard_map/joint/pallas_call | solution.py:366
  18.3 0.6 %spread.1 = (bf16[8,1536]{1,0:T(8,128)(2,1)}, bf16[8,1536]{1,0:T(8,128)(2,1)}) custom-call(bf16[12,16,128]{2,1,0:T(8,128)(2,1)S(1)} %joint.1.o_in), custom_call_target="tpu_custom_call" | custom-call | tf_op jit(solution)/shard_map/spread/pallas_call | solution.py:392

commit v8 on v7

--- a/solution.py
+++ b/solution.py
@@ -24,8 +24,8 @@
 OWNERS = (
     [at(0, 0, 0), at(1, 0, 0), at(0, 0, 1), at(0, 1, 0), at(3, 0, 0), at(1, 0, 1),
      at(0, 0, 2), at(2, 0, 0), at(1, 1, 0), at(2, 0, 1), at(0, 1, 1), at(0, 0, 3)],
-    [at(3, 0, 1), at(1, 0, 2), at(1, 0, 3), at(2, 1, 0), at(2, 0, 2), at(3, 1, 0),
-     at(0, 1, 2), at(1, 1, 1), at(0, 1, 3), at(2, 0, 3), at(1, 1, 2), at(0, 3, 0)],
+    [at(3, 0, 1), at(1, 0, 2), at(1, 0, 3), at(2, 1, 0), at(3, 1, 1), at(3, 1, 0),
+     at(0, 1, 2), at(1, 1, 1), at(0, 1, 3), at(1, 1, 3), at(0, 2, 0), at(0, 3, 0)],
 )
 HOME = set(OWNERS[1])
 

time: 19.1 us -> 18.6 us (0.974)
  Pallas kernels: 17.6 us -> 17.2 us
    pallas_call x1, Pallas kernels: 17 us -> 16.5 us  [local(): pl.pallas_call(kernel, out_shape=pltpu.VMEM((HEADS, 2 * ROWS, HD), bf16),...]
where the time goes in v8:
time: 18.6 us; the launch traced here: 18.4 us
  Pallas kernels  17.2 us (92%)
  between operations  1.29 us (7%)
    pallas_call x1, Pallas kernels, local(): pl.pallas_call(kernel, out_shape=pltpu.VMEM((HEADS, 2 * ROWS, HD), bf16),...  16.5 us
    pallas_call x1, Pallas kernels, local(): pl.pallas_call(spread, out_shape=(out, out), in_specs=[vmem], out_specs=(...  0.63 us

profile of v8, /device:TPU:1, one launch (start us, length us, event | category | flops | bytes accessed | tf_op | source)
XLA Modules:
  0.0 18.4 jit_solution(15640339673024643926)
XLA Ops:
  1.3 16.5 %joint.1.o_in = bf16[12,16,128]{2,1,0:T(8,128)(2,1)S(1)} custom-call(s32[8]{0:T(128)} %order_hbm.1, s32[1]{0:T(128)S(6)} %copy.14.length_hbm, bf16[8,1536]{1,0:T(8,128)(2,1)} %iq_hbm.1, bf16[8,1536]{1,0:T(8,128)(2,1)} %ik_hbm.1, bf16[8,1536]{1,0:T(8,128)(2,1)} %iv_hbm.1, bf16[512,1536]{1,0:T(8,128)(2,1)} %tq_hbm.1, bf16[512,1536]{1,0:T(8,128)(2,1)} %tk_hbm.1, ...), custom_call_target="tpu_custom_call" | custom-call | tf_op jit(solution)/shard_map/joint/pallas_call | solution.py:366
  17.8 0.6 %spread.1 = (bf16[8,1536]{1,0:T(8,128)(2,1)}, bf16[8,1536]{1,0:T(8,128)(2,1)}) custom-call(bf16[12,16,128]{2,1,0:T(8,128)(2,1)S(1)} %joint.1.o_in), custom_call_target="tpu_custom_call" | custom-call | tf_op jit(solution)/shard_map/spread/pallas_call | solution.py:392

commit v9 on v8

--- a/solution.py
+++ b/solution.py
@@ -304,7 +304,7 @@
                 image, text = o[:half].reshape(PLANE, ROWS, HD), o[half:].reshape(PLANE, ROWS, HD)
                 o_out[pl.ds(group * PLANE, PLANE)] = jnp.concatenate([image, text], axis=1).astype(jnp.bfloat16)
             with jax.named_scope("n%d_send" % group):
-                for i in range(PLANE):
+                for i in (0, 12, 8, 4, 1, 13, 3, 15, 9, 11, 5, 7, 2, 14, 10, 6):
                     to = at(i // 4, group, i % 4)
 
                     def send():
@@ -344,13 +344,10 @@
 
 
 def spread(o_in, image_hbm, text_hbm, image, text, sem):
-    for h in range(HEADS):
-        o = o_in[h].astype(jnp.float32)
-        cols = slice(h * HD, (h + 1) * HD)
-        image[:, cols] = o[:ROWS].astype(jnp.bfloat16)
-        text[:, cols] = o[ROWS:].astype(jnp.bfloat16)
-    pltpu.make_async_copy(image, image_hbm, sem).start()
-    pltpu.make_async_copy(text, text_hbm, sem).start()
+    for block, block_hbm, rows in ((image, image_hbm, slice(0, ROWS)), (text, text_hbm, slice(ROWS, 2 * ROWS))):
+        for h in range(HEADS):
+            block[:, h * HD:(h + 1) * HD] = o_in[h].astype(jnp.float32)[rows].astype(jnp.bfloat16)
+        pltpu.make_async_copy(block, block_hbm, sem).start()
     pltpu.make_async_copy(o_in, o_in, sem).wait()
 
 

time: 18.6 us -> 18.6 us (level)
  no operation moved by 1% of the time
where the time goes in v9:
time: 18.6 us; the launch traced here: 18.4 us
  Pallas kernels  17.2 us (92%)
  between operations  1.29 us (7%)
    pallas_call x1, Pallas kernels, local(): pl.pallas_call(kernel, out_shape=pltpu.VMEM((HEADS, 2 * ROWS, HD), bf16),...  16.5 us
    pallas_call x1, Pallas kernels, local(): pl.pallas_call(spread, out_shape=(out, out), in_specs=[vmem], out_specs=(...  0.63 us

profile of v9, /device:TPU:1, one launch (start us, length us, event | category | flops | bytes accessed | tf_op | source)
XLA Modules:
  0.0 18.4 jit_solution(18345976397839392305)
XLA Ops:
  1.3 16.5 %joint.1.o_in = bf16[12,16,128]{2,1,0:T(8,128)(2,1)S(1)} custom-call(s32[8]{0:T(128)} %order_hbm.1, s32[1]{0:T(128)S(6)} %copy.14.length_hbm, bf16[8,1536]{1,0:T(8,128)(2,1)} %iq_hbm.1, bf16[8,1536]{1,0:T(8,128)(2,1)} %ik_hbm.1, bf16[8,1536]{1,0:T(8,128)(2,1)} %iv_hbm.1, bf16[512,1536]{1,0:T(8,128)(2,1)} %tq_hbm.1, bf16[512,1536]{1,0:T(8,128)(2,1)} %tk_hbm.1, ...), custom_call_target="tpu_custom_call" | custom-call | tf_op jit(solution)/shard_map/joint/pallas_call | solution.py:363
  17.8 0.6 %spread.1 = (bf16[8,1536]{1,0:T(8,128)(2,1)}, bf16[8,1536]{1,0:T(8,128)(2,1)}) custom-call(bf16[12,16,128]{2,1,0:T(8,128)(2,1)S(1)} %joint.1.o_in), custom_call_target="tpu_custom_call" | custom-call | tf_op jit(solution)/shard_map/spread/pallas_call | solution.py:389

commit v10 on v9

--- a/solution.py
+++ b/solution.py
@@ -24,7 +24,7 @@
 OWNERS = (
     [at(0, 0, 0), at(1, 0, 0), at(0, 0, 1), at(0, 1, 0), at(3, 0, 0), at(1, 0, 1),
      at(0, 0, 2), at(2, 0, 0), at(1, 1, 0), at(2, 0, 1), at(0, 1, 1), at(0, 0, 3)],
-    [at(3, 0, 1), at(1, 0, 2), at(1, 0, 3), at(2, 1, 0), at(3, 1, 1), at(3, 1, 0),
+    [at(3, 0, 1), at(1, 0, 2), at(1, 2, 0), at(2, 1, 0), at(3, 1, 1), at(3, 1, 0),
      at(0, 1, 2), at(1, 1, 1), at(0, 1, 3), at(1, 1, 3), at(0, 2, 0), at(0, 3, 0)],
 )
 HOME = set(OWNERS[1])

time: 18.6 us -> 18.6 us (level)
  no operation moved by 1% of the time
where the time goes in v10:
time: 18.6 us; the launch traced here: 18.4 us
  Pallas kernels  17.2 us (92%)
  between operations  1.29 us (7%)
    pallas_call x1, Pallas kernels, local(): pl.pallas_call(kernel, out_shape=pltpu.VMEM((HEADS, 2 * ROWS, HD), bf16),...  16.5 us
    pallas_call x1, Pallas kernels, local(): pl.pallas_call(spread, out_shape=(out, out), in_specs=[vmem], out_specs=(...  0.63 us

profile of v10, /device:TPU:1, one launch (start us, length us, event | category | flops | bytes accessed | tf_op | source)
XLA Modules:
  0.0 18.4 jit_solution(10658584671465754180)
XLA Ops:
  1.3 16.5 %joint.1.o_in = bf16[12,16,128]{2,1,0:T(8,128)(2,1)S(1)} custom-call(s32[8]{0:T(128)} %order_hbm.1, s32[1]{0:T(128)S(6)} %copy.14.length_hbm, bf16[8,1536]{1,0:T(8,128)(2,1)} %iq_hbm.1, bf16[8,1536]{1,0:T(8,128)(2,1)} %ik_hbm.1, bf16[8,1536]{1,0:T(8,128)(2,1)} %iv_hbm.1, bf16[512,1536]{1,0:T(8,128)(2,1)} %tq_hbm.1, bf16[512,1536]{1,0:T(8,128)(2,1)} %tk_hbm.1, ...), custom_call_target="tpu_custom_call" | custom-call | tf_op jit(solution)/shard_map/joint/pallas_call | solution.py:363
  17.8 0.6 %spread.1 = (bf16[8,1536]{1,0:T(8,128)(2,1)}, bf16[8,1536]{1,0:T(8,128)(2,1)}) custom-call(bf16[12,16,128]{2,1,0:T(8,128)(2,1)S(1)} %joint.1.o_in), custom_call_target="tpu_custom_call" | custom-call | tf_op jit(solution)/shard_map/spread/pallas_call | solution.py:389
